TPU v7x, 512 devices: a whole 4x4x16 slice. The times are simulated.
512 devices in a mesh: task: 4 (over z_hi, core), seq: 16 (over x, y), dp: 8 (over z_lo).
Axes of the slice: x: 4, y: 4, z: 16 (z_hi: 2, z_lo: 8; z = z_hi * 8 + z_lo), core: 2. Of those that a mesh axis runs over, the one named last changes fastest.
Arguments:
- enc_grads: bfloat16 [4, 8, 2048, 4096], P('task', 'dp', 'seq'), may hold values from -12 to 12
- hidden: bfloat16 [8, 2048, 4096], P('dp', 'seq', 'task'), may hold values from -900 to 900
- final_gain: float32 [4096], replicated, may hold values from 0.1 to 1.9
- attn_out: bfloat16 [8, 2048, 4096], P('dp', 'seq', 'task'), may hold values from -6 to 6
- qkv: bfloat16 [8, 2048, 64, 192], P('dp', None, ('task', 'seq')), may hold values from -48 to 48
- out_weight: bfloat16 [4096, 4096], P('task', ('seq', 'dp')), may hold values from -0.09375 to 0.09375
- doc_lengths: int32 [8], P('dp'), may hold values from 512 to 2048
Outputs:
- resid_grad: bfloat16 [8, 2048, 4096], P('dp', 'seq', 'task')
- qkv_grad: bfloat16 [8, 2048, 64, 192], P('dp', None, ('task', 'seq'))
- weight_grad: float32 [4096, 4096], P('task', ('seq', 'dp'))
Inputs may be any that keep to these rules, and one draw needn't show every extreme that they name: `doc_lengths`: positions at or after a document's length are padding and are never attended to as keys.
All inputs are finite; a program needn't handle non-finite values.
Results may differ from a plain program's by a relative error of at most 0.02.
Values may be sent and summed in bfloat16 or wider, within the bound.
No kernel may reach another device: no remote copies, remote signals or barrier semaphores. Data moves between devices by JAX's collectives and lax.ppermute only.
A program may use at most 64 MiB of HBM per device.

v0:
```python
import jax
import jax.numpy as jnp
from jax import lax
from jax.sharding import PartitionSpec as P

eps_norm = 1e-06


def split_up(shard, dim, peers):
    lengths = shard.shape
    pieces = shard.reshape(*lengths[:dim], peers, lengths[dim] // peers, *lengths[dim + 1 :])
    return jnp.moveaxis(pieces, dim, 0)


def sent_and_summed(shard, axis, dim):
    pieces = split_up(shard, dim, lax.axis_size(axis))
    arrived = lax.all_to_all(pieces, axis, split_axis=0, concat_axis=0, tiled=True)
    return arrived.astype(jnp.float32).sum(axis=0)


def copy_for_each(shard, axis):
    copies = jnp.broadcast_to(shard, (lax.axis_size(axis), *shard.shape))
    return lax.all_to_all(copies, axis, split_axis=0, concat_axis=0, tiled=True)


def over_copies(shard, axis):
    everything = copy_for_each(shard, axis)
    return jnp.sum(everything, axis=0)


def packed_total(arrays, axis):
    ends = [0]
    for a in arrays:
        ends.append(ends[-1] + a.size)
    running = over_copies(jnp.concatenate([a.ravel() for a in arrays]), axis)
    return tuple((running[b:e].reshape(a.shape) for a, b, e in zip(arrays, ends, ends[1:])))


def joined_along(pieces, dim):
    lengths = list(pieces.shape[1:])
    lengths[dim] *= pieces.shape[0]
    return jnp.moveaxis(pieces, 0, dim).reshape(lengths)


def gather_directly(shard, axis, dim):
    return joined_along(copy_for_each(shard, axis), dim)


def on_device(enc_grads, hidden, final_gain, attn_out, qkv, out_weight, doc_lengths):
    feature_cols = enc_grads.shape[3]
    task_count = lax.axis_size("task")
    task_pos = lax.axis_index("task")
    share_cols = feature_cols // task_count
    partial_terms = enc_grads[0, 0].astype(jnp.float32)
    summed = sent_and_summed(partial_terms.astype(jnp.bfloat16), "task", 1)
    rows_part = hidden[0].astype(jnp.float32)
    gain_part = lax.dynamic_slice_in_dim(final_gain, task_pos * share_cols, share_cols, 0)
    squares, cross_sum = packed_total(
        (jnp.sum(rows_part * rows_part, axis=-1), jnp.sum(gain_part * summed * rows_part, axis=-1)),
        "task",
    )
    scale_inv = lax.rsqrt(squares / feature_cols + eps_norm)[:, None]
    cross_mean = cross_sum[:, None] * scale_inv / feature_cols
    resid_part = (scale_inv * (gain_part * summed - rows_part * scale_inv * cross_mean)).astype(
        jnp.bfloat16
    )
    resid_full = gather_directly(resid_part, "task", 1)
    weight_slab = gather_directly(out_weight, "dp", 1)
    resid_slice = resid_full
    head_grad = lax.dot_general(
        resid_slice,
        lax.all_gather(weight_slab, "seq", axis=1, tiled=True),
        (((1,), (1,)), ((), ())),
        preferred_element_type=jnp.float32,
    )
    head_grad = head_grad.astype(jnp.bfloat16)
    saved_tok = attn_out[0]
    out_heads, saved_heads = (
        lax.all_to_all(head_grad, "seq", split_axis=1, concat_axis=0, tiled=True),
        lax.all_to_all(saved_tok, "seq", split_axis=1, concat_axis=0, tiled=True),
    )
    resid_cols = lax.all_to_all(resid_full, "seq", split_axis=1, concat_axis=0, tiled=True)
    resid_slice = resid_cols
    grad_block = lax.dot_general(
        lax.all_gather(saved_tok, "seq", axis=0, tiled=True),
        resid_slice,
        (((0,), (0,)), ((), ())),
        preferred_element_type=jnp.float32,
    )
    seq_len = qkv.shape[1]
    weight_grad = sent_and_summed(grad_block.astype(jnp.bfloat16), "dp", 1)
    head_size = qkv.shape[3] // 3
    doc_length = doc_lengths[0]
    key_valid = (jnp.arange(seq_len, dtype=jnp.int32) < doc_length)[None, :]
    block_rows = min(512, seq_len)
    block_count = seq_len // block_rows
    query = qkv[0, :, 0, :head_size]
    key_rows = qkv[0, :, 0, head_size : 2 * head_size]
    value_rows = qkv[0, :, 0, 2 * head_size :]
    delta_rows = jnp.sum(out_heads.astype(jnp.float32) * saved_heads.astype(jnp.float32), axis=-1)

    def block_step(state_pair, block_index):
        key_acc, value_acc = state_pair
        row_start = block_index * block_rows
        query_blk = lax.dynamic_slice_in_dim(query, row_start, block_rows, 0)
        upstream_blk = lax.dynamic_slice_in_dim(out_heads, row_start, block_rows, 0)
        delta_blk = lax.dynamic_slice_in_dim(delta_rows, row_start, block_rows, 0)
        scores = lax.dot_general(
            query_blk, key_rows, (((1,), (1,)), ((), ())), preferred_element_type=jnp.float32
        )
        scores = jnp.where(key_valid, scores, -1e30)
        row_max = jnp.max(scores, axis=-1, keepdims=True)
        expo_terms = jnp.exp(scores - row_max)
        prob_rows = expo_terms / jnp.sum(expo_terms, axis=-1, keepdims=True)
        prob_bf16 = prob_rows.astype(jnp.bfloat16)
        value_acc = value_acc + lax.dot_general(
            prob_bf16, upstream_blk, (((0,), (0,)), ((), ())), preferred_element_type=jnp.float32
        )
        dprob_rows = lax.dot_general(
            upstream_blk, value_rows, (((1,), (1,)), ((), ())), preferred_element_type=jnp.float32
        )
        dscore_rows = (prob_rows * (dprob_rows - delta_blk[:, None])).astype(jnp.bfloat16)
        dquery = jnp.dot(dscore_rows, key_rows, preferred_element_type=jnp.float32).astype(
            jnp.bfloat16
        )
        key_acc = key_acc + lax.dot_general(
            dscore_rows, query_blk, (((0,), (0,)), ((), ())), preferred_element_type=jnp.float32
        )
        return ((key_acc, value_acc), dquery)

    zero_pair = (
        jnp.zeros((seq_len, head_size), jnp.float32),
        jnp.zeros((seq_len, head_size), jnp.float32),
    )
    (key_acc, value_acc), dq_blocks = lax.scan(
        block_step, zero_pair, jnp.arange(block_count, dtype=jnp.int32)
    )
    dquery_all = dq_blocks.reshape(seq_len, head_size)
    head_grads = [
        jnp.concatenate(
            [dquery_all, key_acc.astype(jnp.bfloat16), value_acc.astype(jnp.bfloat16)], axis=-1
        )
    ]
    qkv_grad = jnp.stack(head_grads, axis=1)[None]
    return (resid_part[None], qkv_grad, weight_grad)


def solution(mesh):
    return jax.shard_map(
        on_device,
        mesh=mesh,
        in_specs=(
            P("task", "dp", "seq", None),
            P("dp", "seq", "task"),
            P(),
            P("dp", "seq", "task"),
            P("dp", None, ("task", "seq"), None),
            P("task", ("seq", "dp")),
            P("dp"),
        ),
        out_specs=(
            P("dp", "seq", "task"),
            P("dp", None, ("task", "seq"), None),
            P("task", ("seq", "dp")),
        ),
        check_vma=False,
    )
```

profile of v0, /device:TPU:8, one launch (start us, length us, event | category | flops | bytes accessed | tf_op | source)
XLA Modules:
  0.0 326.9 jit_solution(1640961790241758674)
XLA Ops:
  8.8 41.2 %all_to_all.77 = bf16[8,1024,32]{1,2,0:T(8,128)(2,1)} all-to-all(bf16[8,1024,32]{1,2,0:T(8,128)(2,1)S(1)} %broadcast_in_dim.42), channel_id=1, replica_groups=mesh['task'=4,'seq'=16,'dp'=8] {'dp'}, dimensions={0} | all-to-all | bytes 1048576 | tf_op jit(solution)/shard_map/all_to_all | solution.py:23
  50.0 1.7 copy.68
  53.1 7.6 %all-to-all-start = ((bf16[4,128,1024]{2,1,0:T(8,128)(2,1)}), bf16[4,128,1024]{2,1,0:T(8,128)(2,1)S(1)}, u32[]{:S(2)}, u32[]{:S(2)}) async-start(bf16[4,128,1024]{2,1,0:T(8,128)(2,1)} %copy.69), calls=%async_computation | async-start | bytes 2097152 | tf_op jit(solution)/shard_map/all_to_all | solution.py:17
  61.3 44.1 %all-to-all-done = bf16[4,128,1024]{2,1,0:T(8,128)(2,1)S(1)} async-done(((bf16[4,128,1024]{2,1,0:T(8,128)(2,1)}), bf16[4,128,1024]{2,1,0:T(8,128)(2,1)S(1)}, u32[]{:S(2)}, u32[]{:S(2)}) %all-to-all-start) | async-done | bytes 1048608 | tf_op jit(solution)/shard_map/all_to_all | solution.py:17
  105.8 14.8 %all_to_all.78 = f32[4,1,256]{2,1,0:T(1,128)S(1)} all-to-all(f32[4,1,256]{2,1,0:T(1,128)S(1)} %broadcast_in_dim.39), channel_id=1, replica_groups=mesh['task'=4,'seq'=16,'dp'=8] {'task'}, dimensions={0} | all-to-all | bytes 8192 | tf_op jit(solution)/shard_map/all_to_all | solution.py:23
  121.2 30.5 %all_to_all.79 = bf16[4,128,1024]{1,2,0:T(8,128)(2,1)S(1)} all-to-all(bf16[4,128,1024]{1,2,0:T(8,128)(2,1)S(1)} %broadcast_in_dim.41), channel_id=1, replica_groups=mesh['task'=4,'seq'=16,'dp'=8] {'task'}, dimensions={0} | all-to-all | bytes 2097152 | tf_op jit(solution)/shard_map/all_to_all | solution.py:23
  151.8 30.4 %all_to_all.80 = bf16[128,16,256]{0,2,1:T(8,128)(2,1)S(1)} all-to-all(bf16[128,16,256]{0,2,1:T(8,128)(2,1)S(1)} %bitcast.93), channel_id=1, replica_groups=mesh['task'=4,'seq'=16,'dp'=8] {'seq'}, dimensions={1} | all-to-all | bytes 2097152 | tf_op jit(solution)/shard_map/all_to_all | solution.py:82
  183.5 4.6 %fusion.19 = bf16[256,1024]{1,0:T(8,128)(2,1)} fusion(bf16[2048,256]{1,0:T(8,128)(2,1)} %bitcast.100, bf16[1,2048,1024]{2,1,0:T(8,128)(2,1)} %all-gather.6.cloned.1.call-done), kind=kOutput, calls=%fused_computation.25 | convolution fusion | flops 1074003968 | bytes 5767168 | tf_op jit(solution)/shard_map/dot_general | solution.py:84
  188.1 25.5 %all-to-all-start.7 = ((bf16[8,1024,32]{1,2,0:T(8,128)(2,1)}), bf16[8,1024,32]{1,2,0:T(8,128)(2,1)S(1)}, u32[]{:S(2)}, u32[]{:S(2)}) async-start(bf16[8,1024,32]{1,2,0:T(8,128)(2,1)} %bitcast.25), calls=%async_computation.7 | async-start | bytes 1048576 | tf_op jit(solution)/shard_map/all_to_all | solution.py:17
  214.5 4.7 %convolution_convert_fusion.1 = bf16[128,1024]{1,0:T(8,128)(2,1)S(1)} fusion(bf16[128,4096]{0,1:T(8,128)(2,1)S(1)} %bitcast.94, bf16[1024,4096]{0,1:T(8,128)(2,1)} %all-gather.4.cloned.1.call-done), kind=kOutput, calls=%fused_computation.26 | convolution fusion | flops 1073872896 | bytes 9699328 | tf_op jit(solution)/shard_map/dot_general | solution.py:70
  220.0 21.6 %all-to-all-done.7 = bf16[8,1024,32]{1,2,0:T(8,128)(2,1)S(1)} async-done(((bf16[8,1024,32]{1,2,0:T(8,128)(2,1)}), bf16[8,1024,32]{1,2,0:T(8,128)(2,1)S(1)}, u32[]{:S(2)}, u32[]{:S(2)}) %all-to-all-start.7) | async-done | bytes 524320 | tf_op jit(solution)/shard_map/all_to_all | solution.py:17
  241.6 5.1 %all-to-all-start.4 = ((bf16[128,16,64]{0,2,1:T(8,128)(2,1)}), bf16[128,16,64]{0,2,1:T(8,128)(2,1)S(1)}, u32[]{:S(2)}, u32[]{:S(2)}) async-start(bf16[128,16,64]{0,2,1:T(8,128)(2,1)} %bitcast.10), calls=%async_computation.4 | async-start | bytes 524288 | tf_op jit(solution)/shard_map/all_to_all | solution.py:79
  249.4 4.6 %all-to-all-done.4 = bf16[128,16,64]{0,2,1:T(8,128)(2,1)S(1)} async-done(((bf16[128,16,64]{0,2,1:T(8,128)(2,1)}), bf16[128,16,64]{0,2,1:T(8,128)(2,1)S(1)}, u32[]{:S(2)}, u32[]{:S(2)}) %all-to-all-start.4) | async-done | bytes 262176 | tf_op jit(solution)/shard_map/all_to_all | solution.py:79
  254.1 5.1 %all-to-all-start.5 = ((bf16[128,16,64]{0,2,1:T(8,128)(2,1)}), bf16[128,16,64]{0,2,1:T(8,128)(2,1)S(1)}, u32[]{:S(2)}, u32[]{:S(2)}) async-start(bf16[128,16,64]{0,2,1:T(8,128)(2,1)} %bitcast.14), calls=%async_computation.5 | async-start | bytes 524288 | tf_op jit(solution)/shard_map/all_to_all | solution.py:80
  261.1 5.0 %all-to-all-done.5 = bf16[128,16,64]{0,2,1:T(8,128)(2,1)S(1)} async-done(((bf16[128,16,64]{0,2,1:T(8,128)(2,1)}), bf16[128,16,64]{0,2,1:T(8,128)(2,1)S(1)}, u32[]{:S(2)}, u32[]{:S(2)}) %all-to-all-start.5) | async-done | bytes 262176 | tf_op jit(solution)/shard_map/all_to_all | solution.py:80
  266.2 50.8 %while.15 = (s32[]{:T(128)}, f32[2048,64]{0,1:T(8,128)S(1)}, f32[2048,64]{0,1:T(8,128)}, bf16[4,512,64]{1,2,0:T(8,128)(2,1)}, s32[4]{0:T(128)S(1)}, /*index=5*/b...) while((s32[]{:T(128)}, f32[2048,64]{0,1:T(8,128)S(1)}, ...), condition=%wide.region_8.9_spmd.clone, body=%wide.region_5.8_spmd.clone.sunk | while | flops 687375360 | bytes 65895284 | solution.py:135
  269.0 1.9 copy-done
  271.8 3.5 %convolution_add_fusion.5 = f32[2048,64]{0,1:T(8,128)S(1)} fusion(f32[2048,64]{0,1:T(8,128)S(1)} %copy-done.5, pred[]{:T(512)S(6)} %compare.3, bf16[2048,64]{1,0:T(8,128)(2,1)S(1)} %get-tuple-element.298, s32[]{:T(128)S(6)} %select_n.35, f32[512,2048]{1,0:T(8,128)} %copy-done, f32[512]{0:T(512)S(1)} %fusion.65, f32[512]{0:T(512)S(1)} %get-tuple-element.260, ...), kind=kOutput, calls=%fused_computation.6.clone.1 | convolution fusion | flops 138674176 | bytes 5380101 | tf_op jit(solution)/shard_map/while/body/eval_jaxpr/dot_general | solution.py:116
  275.3 1.6 multiply_convert_fusion.2
  277.5 1.4 fusion.66
  281.7 1.9 copy-done
  284.5 3.5 %convolution_add_fusion.5 = f32[2048,64]{0,1:T(8,128)S(1)} fusion(f32[2048,64]{0,1:T(8,128)S(1)} %copy-done.5, pred[]{:T(512)S(6)} %compare.3, bf16[2048,64]{1,0:T(8,128)(2,1)S(1)} %get-tuple-element.298, s32[]{:T(128)S(6)} %select_n.35, f32[512,2048]{1,0:T(8,128)} %copy-done, f32[512]{0:T(512)S(1)} %fusion.65, f32[512]{0:T(512)S(1)} %get-tuple-element.260, ...), kind=kOutput, calls=%fused_computation.6.clone.1 | convolution fusion | flops 138674176 | bytes 5380101 | tf_op jit(solution)/shard_map/while/body/eval_jaxpr/dot_general | solution.py:116
  288.0 1.6 multiply_convert_fusion.2
  290.2 1.4 fusion.66
  294.4 1.9 copy-done
  297.1 3.5 %convolution_add_fusion.5 = f32[2048,64]{0,1:T(8,128)S(1)} fusion(f32[2048,64]{0,1:T(8,128)S(1)} %copy-done.5, pred[]{:T(512)S(6)} %compare.3, bf16[2048,64]{1,0:T(8,128)(2,1)S(1)} %get-tuple-element.298, s32[]{:T(128)S(6)} %select_n.35, f32[512,2048]{1,0:T(8,128)} %copy-done, f32[512]{0:T(512)S(1)} %fusion.65, f32[512]{0:T(512)S(1)} %get-tuple-element.260, ...), kind=kOutput, calls=%fused_computation.6.clone.1 | convolution fusion | flops 138674176 | bytes 5380101 | tf_op jit(solution)/shard_map/while/body/eval_jaxpr/dot_general | solution.py:116
  300.7 1.6 multiply_convert_fusion.2
  302.9 1.4 fusion.66
  307.0 1.9 copy-done
  309.8 3.5 %convolution_add_fusion.5 = f32[2048,64]{0,1:T(8,128)S(1)} fusion(f32[2048,64]{0,1:T(8,128)S(1)} %copy-done.5, pred[]{:T(512)S(6)} %compare.3, bf16[2048,64]{1,0:T(8,128)(2,1)S(1)} %get-tuple-element.298, s32[]{:T(128)S(6)} %select_n.35, f32[512,2048]{1,0:T(8,128)} %copy-done, f32[512]{0:T(512)S(1)} %fusion.65, f32[512]{0:T(512)S(1)} %get-tuple-element.260, ...), kind=kOutput, calls=%fused_computation.6.clone.1 | convolution fusion | flops 138674176 | bytes 5380101 | tf_op jit(solution)/shard_map/while/body/eval_jaxpr/dot_general | solution.py:116
  313.4 1.6 multiply_convert_fusion.2
  315.6 1.4 fusion.66
  (101 shorter events, 29.7 us)
Async XLA Ops:
  7.2 176.3 %all-gather.6.cloned.1.call-start = ((), (), s32[]{:S(2)}) async-start(), calls=%async_computation.9 | async-start | bytes 4456448 | tf_op jit(solution)/shard_map/all_gather | solution.py:85
  7.9 206.6 %all-gather.4.cloned.1.call-start = ((), (), s32[]{:S(2)}) async-start(), calls=%async_computation.8 | async-start | bytes 8912896 | tf_op jit(solution)/shard_map/all_gather | solution.py:72
  50.0 55.6 %copy-start.2 = (bf16[1,128,1024]{2,1,0:T(8,128)(2,1)S(1)}, bf16[1,128,1024]{2,1,0:T(8,128)(2,1)}, u32[]{:S(2)}) copy-start(bf16[1,128,1024]{2,1,0:T(8,128)(2,1)} %param.10) | copy-start | bytes 786436
  53.1 52.4 %all-to-all-start = ((bf16[4,128,1024]{2,1,0:T(8,128)(2,1)}), bf16[4,128,1024]{2,1,0:T(8,128)(2,1)S(1)}, u32[]{:S(2)}, u32[]{:S(2)}) async-start(bf16[4,128,1024]{2,1,0:T(8,128)(2,1)} %copy.69), calls=%async_computation | async-start | bytes 2097152 | tf_op jit(solution)/shard_map/all_to_all | solution.py:17
  183.5 30.1 %copy-start.3 = (bf16[1,128,1024]{2,1,0:T(8,128)(2,1)S(1)}, bf16[1,128,1024]{2,1,0:T(8,128)(2,1)}, u32[]{:S(2)}) copy-start(bf16[1,128,1024]{2,1,0:T(8,128)(2,1)} %param.12) | copy-start | bytes 786436
  188.1 53.5 %all-to-all-start.7 = ((bf16[8,1024,32]{1,2,0:T(8,128)(2,1)}), bf16[8,1024,32]{1,2,0:T(8,128)(2,1)S(1)}, u32[]{:S(2)}, u32[]{:S(2)}) async-start(bf16[8,1024,32]{1,2,0:T(8,128)(2,1)} %bitcast.25), calls=%async_computation.7 | async-start | bytes 1048576 | tf_op jit(solution)/shard_map/all_to_all | solution.py:17
  241.6 12.5 %all-to-all-start.4 = ((bf16[128,16,64]{0,2,1:T(8,128)(2,1)}), bf16[128,16,64]{0,2,1:T(8,128)(2,1)S(1)}, u32[]{:S(2)}, u32[]{:S(2)}) async-start(bf16[128,16,64]{0,2,1:T(8,128)(2,1)} %bitcast.10), calls=%async_computation.4 | async-start | bytes 524288 | tf_op jit(solution)/shard_map/all_to_all | solution.py:79
  254.1 12.1 %all-to-all-start.5 = ((bf16[128,16,64]{0,2,1:T(8,128)(2,1)}), bf16[128,16,64]{0,2,1:T(8,128)(2,1)S(1)}, u32[]{:S(2)}, u32[]{:S(2)}) async-start(bf16[128,16,64]{0,2,1:T(8,128)(2,1)} %bitcast.14), calls=%async_computation.5 | async-start | bytes 524288 | tf_op jit(solution)/shard_map/all_to_all | solution.py:80
  268.2 3.6 %copy-start.5 = (f32[2048,64]{0,1:T(8,128)S(1)}, f32[2048,64]{0,1:T(8,128)}, u32[]{:S(2)}) copy-start(f32[2048,64]{0,1:T(8,128)} %get-tuple-element.278) | copy-start | bytes 1572868 | tf_op jit(solution)/shard_map/while
  269.0 1.9 copy-start
  271.7 3.6 %copy-start.1 = (f32[512,2048]{1,0:T(8,128)S(1)}, f32[512,2048]{1,0:T(8,128)}, u32[]{:S(2)}) copy-start(f32[512,2048]{1,0:T(8,128)} %copy-done) | copy-start | bytes 12582916 | tf_op jit(solution)/shard_map/while
  271.8 3.6 %copy-start.4 = (bf16[2048,64]{1,0:T(8,128)(2,1)S(1)}, bf16[2048,64]{1,0:T(8,128)(2,1)}, u32[]{:S(2)}) copy-start(bf16[2048,64]{1,0:T(8,128)(2,1)} %get-tuple-element.299) | copy-start | bytes 786436 | tf_op jit(solution)/shard_map/while
  275.2 1.7 copy-start.6
  280.9 3.6 %copy-start.5 = (f32[2048,64]{0,1:T(8,128)S(1)}, f32[2048,64]{0,1:T(8,128)}, u32[]{:S(2)}) copy-start(f32[2048,64]{0,1:T(8,128)} %get-tuple-element.278) | copy-start | bytes 1572868 | tf_op jit(solution)/shard_map/while
  281.7 1.9 copy-start
  284.4 3.6 %copy-start.1 = (f32[512,2048]{1,0:T(8,128)S(1)}, f32[512,2048]{1,0:T(8,128)}, u32[]{:S(2)}) copy-start(f32[512,2048]{1,0:T(8,128)} %copy-done) | copy-start | bytes 12582916 | tf_op jit(solution)/shard_map/while
  284.5 3.6 %copy-start.4 = (bf16[2048,64]{1,0:T(8,128)(2,1)S(1)}, bf16[2048,64]{1,0:T(8,128)(2,1)}, u32[]{:S(2)}) copy-start(bf16[2048,64]{1,0:T(8,128)(2,1)} %get-tuple-element.299) | copy-start | bytes 786436 | tf_op jit(solution)/shard_map/while
  287.9 1.7 copy-start.6
  293.6 3.6 %copy-start.5 = (f32[2048,64]{0,1:T(8,128)S(1)}, f32[2048,64]{0,1:T(8,128)}, u32[]{:S(2)}) copy-start(f32[2048,64]{0,1:T(8,128)} %get-tuple-element.278) | copy-start | bytes 1572868 | tf_op jit(solution)/shard_map/while
  294.4 1.9 copy-start
  297.1 3.6 %copy-start.1 = (f32[512,2048]{1,0:T(8,128)S(1)}, f32[512,2048]{1,0:T(8,128)}, u32[]{:S(2)}) copy-start(f32[512,2048]{1,0:T(8,128)} %copy-done) | copy-start | bytes 12582916 | tf_op jit(solution)/shard_map/while
  297.1 3.6 %copy-start.4 = (bf16[2048,64]{1,0:T(8,128)(2,1)S(1)}, bf16[2048,64]{1,0:T(8,128)(2,1)}, u32[]{:S(2)}) copy-start(bf16[2048,64]{1,0:T(8,128)(2,1)} %get-tuple-element.299) | copy-start | bytes 786436 | tf_op jit(solution)/shard_map/while
  300.6 1.7 copy-start.6
  306.2 3.6 %copy-start.5 = (f32[2048,64]{0,1:T(8,128)S(1)}, f32[2048,64]{0,1:T(8,128)}, u32[]{:S(2)}) copy-start(f32[2048,64]{0,1:T(8,128)} %get-tuple-element.278) | copy-start | bytes 1572868 | tf_op jit(solution)/shard_map/while
  307.0 1.9 copy-start
  309.8 3.6 %copy-start.1 = (f32[512,2048]{1,0:T(8,128)S(1)}, f32[512,2048]{1,0:T(8,128)}, u32[]{:S(2)}) copy-start(f32[512,2048]{1,0:T(8,128)} %copy-done) | copy-start | bytes 12582916 | tf_op jit(solution)/shard_map/while
  309.8 3.6 %copy-start.4 = (bf16[2048,64]{1,0:T(8,128)(2,1)S(1)}, bf16[2048,64]{1,0:T(8,128)(2,1)}, u32[]{:S(2)}) copy-start(bf16[2048,64]{1,0:T(8,128)(2,1)} %get-tuple-element.299) | copy-start | bytes 786436 | tf_op jit(solution)/shard_map/while
  313.3 1.7 copy-start.6
Sparse Core Ops, SparseCore 0:
  11.0 70.9 all-gather.5
  85.0 96.0 all-gather.3
where the time goes:
time: 328 us; the launch traced here: 327 us
  blocking collectives  117 us (36%)
  waiting for transfers between devices  76.1 us (23%)
  starting transfers between devices  43.4 us (13%)
  matrix products  40.7 us (12%)
  local copies, waits for them, and re-layouts  22.4 us (7%)
  between operations  14.2 us (4%)
  other arithmetic  10.4 us (3%)
    all_to_all x3, blocking collectives, copy_for_each(): return lax.all_to_all(copies, axis, split_axis=0, concat_axis=0, tiled=True)  86.5 us
    all_to_all x2, waiting for transfers between devices, sent_and_summed(): lax.all_to_all(pieces, axis, split_axis=0, concat_axis=0, tiled=True)  65.7 us
    all_to_all x2, starting transfers between devices, sent_and_summed(): lax.all_to_all(pieces, axis, split_axis=0, concat_axis=0, tiled=True)  33.1 us
    all_to_all x1, blocking collectives, on_device(): lax.all_to_all(resid_full, 'seq', split_axis=1, concat_axis=0, tiled=True)  30.4 us
    dot_general x4, matrix products, block_step(): lax.dot_general(prob_bf16, upstream_blk, (((0,), (0,)), ((), ())), prefer...  13.8 us
    while x40, local copies, waits for them, and re-layouts  7.78 us
  transfers between devices with their start and end apart: 6, of which 4 were waited for; matrix products, arithmetic and copies ran while one was open for 7% of the time, Pallas kernels for 0%

commit v1 on v0

v1 whole, which is shorter than its diff:
```python
import jax
import jax.numpy as jnp
from jax import lax
from jax.experimental import pallas as pl
from jax.experimental.pallas import tpu as pltpu
from jax.sharding import PartitionSpec as P


eps_norm = 1e-06
core_swap = [(0, 1), (1, 0), (2, 3), (3, 2)]
far_swap = [(0, 2), (2, 0), (1, 3), (3, 1)]
corner_swap = [(0, 3), (3, 0), (1, 2), (2, 1)]
NT = (((1,), (1,)), ((), ()))
NN = (((1,), (0,)), ((), ()))
tile = 256


def probs_kernel(length_ref, q_ref, k_ref, out_ref, held):
    keys = k_ref.shape[0]
    q = q_ref[...]
    length = length_ref[0]
    top = None
    for start in range(0, keys, tile):
        rows = pl.ds(start, tile)
        s = lax.dot_general(k_ref[rows, :], q, NT, preferred_element_type=jnp.float32)
        place = lax.broadcasted_iota(jnp.int32, s.shape, 0) + start
        s = jnp.where(place < length, s, -1e30)
        held[rows, :] = s
        peak = jnp.max(s, axis=0, keepdims=True)
        top = peak if top is None else jnp.maximum(top, peak)
    total = jnp.zeros_like(top)
    for start in range(0, keys, tile):
        rows = pl.ds(start, tile)
        e = jnp.exp(held[rows, :] - top)
        held[rows, :] = e
        total = total + jnp.sum(e, axis=0, keepdims=True)
    share = 1.0 / total
    for start in range(0, keys, tile):
        rows = pl.ds(start, tile)
        out_ref[rows, :] = (held[rows, :] * share).astype(out_ref.dtype)


def probs_of(length, query, key_rows):
    n, size = query.shape
    return pl.pallas_call(
        probs_kernel,
        grid=(n // tile,),
        in_specs=[
            pl.BlockSpec(memory_space=pltpu.SMEM),
            pl.BlockSpec((tile, size), lambda i: (i, 0)),
            pl.BlockSpec((n, size), lambda i: (0, 0)),
        ],
        out_specs=pl.BlockSpec((n, tile), lambda i: (0, i)),
        out_shape=jax.ShapeDtypeStruct((n, n), jnp.bfloat16),
        scratch_shapes=[pltpu.VMEM((n, tile), jnp.float32)],
        cost_estimate=pl.CostEstimate(
            flops=8 * n * n * size, bytes_accessed=2 * n * n, transcendentals=n * n
        ),
        name="probs",
    )(length, query, key_rows)


def grads_kernel(p_ref, q_ref, g_ref, o_ref, k_ref, v_ref, kt_ref, out_ref, dk_acc, dv_acc):
    i = pl.program_id(0)
    keys, size = k_ref.shape
    q = q_ref[...]
    g = g_ref[...]
    prod = g.astype(jnp.float32) * o_ref[...].astype(jnp.float32)
    delta = lax.dot_general(
        jnp.ones((8, size), jnp.float32),
        prod,
        NT,
        precision=lax.Precision.HIGHEST,
        preferred_element_type=jnp.float32,
    )[0:1, :]

    @pl.when(i == 0)
    def _():
        dk_acc[...] = jnp.zeros_like(dk_acc)
        dv_acc[...] = jnp.zeros_like(dv_acc)

    dqt = jnp.zeros((size, tile), jnp.float32)
    for start in range(0, keys, tile):
        rows = pl.ds(start, tile)
        p = p_ref[rows, :]
        dp = lax.dot_general(v_ref[rows, :], g, NT, preferred_element_type=jnp.float32)
        ds = (p.astype(jnp.float32) * (dp - delta)).astype(jnp.bfloat16)
        dv_acc[rows, :] += lax.dot_general(p, g, NN, preferred_element_type=jnp.float32)
        dk_acc[rows, :] += lax.dot_general(ds, q, NN, preferred_element_type=jnp.float32)
        dqt = dqt + lax.dot_general(kt_ref[:, rows], ds, NN, preferred_element_type=jnp.float32)
    out_ref[pl.ds(pl.multiple_of(i * tile, tile), tile), 0:size] = dqt.T.astype(out_ref.dtype)

    @pl.when(i == pl.num_programs(0) - 1)
    def _():
        out_ref[:, size : 2 * size] = dk_acc[...].astype(out_ref.dtype)
        out_ref[:, 2 * size :] = dv_acc[...].astype(out_ref.dtype)


def grads_of(probs, query, upstream, saved, key_rows, value_rows, key_cols):
    n, size = query.shape
    part = pl.BlockSpec((tile, size), lambda i: (i, 0))
    whole = pl.BlockSpec((n, size), lambda i: (0, 0))
    return pl.pallas_call(
        grads_kernel,
        grid=(n // tile,),
        in_specs=[
            pl.BlockSpec((n, tile), lambda i: (0, i)),
            part,
            part,
            part,
            whole,
            whole,
            pl.BlockSpec((size, n), lambda i: (0, 0)),
        ],
        out_specs=pl.BlockSpec((n, 3 * size), lambda i: (0, 0)),
        out_shape=jax.ShapeDtypeStruct((n, 3 * size), jnp.bfloat16),
        scratch_shapes=[pltpu.VMEM((n, size), jnp.float32), pltpu.VMEM((n, size), jnp.float32)],
        cost_estimate=pl.CostEstimate(
            flops=8 * n * n * size, bytes_accessed=2 * n * n, transcendentals=0
        ),
        name="grads",
    )(probs, query, upstream, saved, key_rows, value_rows, key_cols)


def copy_for_each(shard, axis):
    copies = jnp.broadcast_to(shard, (lax.axis_size(axis), *shard.shape))
    return lax.all_to_all(copies, axis, split_axis=0, concat_axis=0, tiled=True)


def pick(stack, index):
    return lax.dynamic_index_in_dim(stack, index, 0, keepdims=False)


def compute(enc_grads, hidden, final_gain, attn_out, qkv, out_weight, doc_lengths):
    rows, feature_cols = enc_grads.shape[2:]
    tasks = lax.axis_size("task")
    task_pos = lax.axis_index("task")
    far, core = task_pos // 2, task_pos % 2
    share_cols = feature_cols // tasks
    dp_count = lax.axis_size("dp")
    seq_len = qkv.shape[1]
    head_size = qkv.shape[3] // 3

    heads = qkv.reshape(seq_len, 3 * head_size)
    query = heads[:, :head_size]
    key_rows = heads[:, head_size : 2 * head_size]
    value_rows = heads[:, 2 * head_size :]
    probs = probs_of(doc_lengths, query, key_rows)

    slab = copy_for_each(out_weight.T, "dp")
    slab = slab.reshape(-1, slab.shape[-1])
    terms = enc_grads[0, 0].reshape(rows, 2, 2, share_cols)
    kept = jnp.where(core == 0, terms[:, :, 0], terms[:, :, 1])
    given = jnp.where(core == 0, terms[:, :, 1], terms[:, :, 0])
    came = lax.ppermute(given, "task", core_swap)
    pair = kept.astype(jnp.float32) + came.astype(jnp.float32)
    mine = jnp.where(far == 0, pair[:, 0], pair[:, 1])
    theirs = jnp.where(far == 0, pair[:, 1], pair[:, 0])
    came = lax.ppermute(theirs.astype(jnp.bfloat16), "task", far_swap)
    summed = mine + came.astype(jnp.float32)

    saved_tok, slab = lax.optimization_barrier((attn_out[0], slab))
    saved_all = copy_for_each(saved_tok, "seq")
    saved_all = saved_all.reshape(seq_len, -1)
    weight = lax.all_gather(slab, "seq", axis=0, tiled=True)

    stream = hidden[0].astype(jnp.float32)
    gain = lax.dynamic_slice_in_dim(final_gain, task_pos * share_cols, share_cols, 0)
    sums = jnp.concatenate(
        [jnp.sum(stream * stream, axis=-1), jnp.sum(gain * summed * stream, axis=-1)]
    )
    sums = sums[None]
    shares = [sums]
    for pairs in (core_swap, far_swap, corner_swap):
        shares.append(lax.ppermute(sums, "task", pairs))
    sums = (shares[0] + shares[1] + shares[2] + shares[3])[0]
    squares, cross_sum = sums[:rows], sums[rows:]
    scale_inv = lax.rsqrt(squares / feature_cols + eps_norm)[:, None]
    cross_mean = cross_sum[:, None] * scale_inv / feature_cols
    resid = (scale_inv * (gain * summed - stream * scale_inv * cross_mean)).astype(jnp.bfloat16)

    beside = lax.ppermute(resid, "task", core_swap)
    across = lax.ppermute(resid, "task", far_swap)
    corner = lax.ppermute(across, "task", core_swap)
    near_first = jnp.where(core == 0, resid, beside)
    near_second = jnp.where(core == 0, beside, resid)
    far_first = jnp.where(core == 0, across, corner)
    far_second = jnp.where(core == 0, corner, across)
    resid_full = jnp.concatenate(
        [
            jnp.where(far == 0, near_first, far_first),
            jnp.where(far == 0, near_second, far_second),
            jnp.where(far == 0, far_first, near_first),
            jnp.where(far == 0, far_second, near_second),
        ],
        axis=1,
    )

    resid_full, saved_all = lax.optimization_barrier((resid_full, saved_all))
    resid_cols = lax.all_to_all(resid_full, "seq", split_axis=1, concat_axis=0, tiled=True)
    grad_block = lax.dot_general(
        resid_cols, saved_all, (((0,), (0,)), ((), ())), preferred_element_type=jnp.float32
    )
    blocks = grad_block.reshape(dp_count, -1, grad_block.shape[-1])
    sent = blocks.astype(jnp.bfloat16)
    dp_pos = lax.axis_index("dp")
    weight_sum = pick(blocks, dp_pos)
    for step in range(1, dp_count):
        ring = [(d, (d + step) % dp_count) for d in range(dp_count)]
        piece = pick(sent, (dp_pos + step) % dp_count)
        piece = lax.ppermute(piece, "dp", ring)
        weight_sum = weight_sum + piece.astype(jnp.float32)
    weight_grad = weight_sum.T

    head_grad = lax.dot_general(
        resid_full, weight, NN, preferred_element_type=jnp.float32
    ).astype(jnp.bfloat16)
    head_grad, resid_cols = lax.optimization_barrier((head_grad, resid_cols))
    upstream = lax.all_to_all(head_grad, "seq", split_axis=1, concat_axis=0, tiled=True)
    saved = lax.dynamic_slice_in_dim(
        saved_all, lax.axis_index("seq") * head_size, head_size, 1
    )
    qkv_grad = grads_of(probs, query, upstream, saved, key_rows, value_rows, key_rows.T)
    return (resid[None], qkv_grad.reshape(1, seq_len, 1, 3 * head_size), weight_grad)


def solution(mesh):
    return jax.shard_map(
        compute,
        mesh=mesh,
        in_specs=(
            P("task", "dp", "seq", None),
            P("dp", "seq", "task"),
            P(),
            P("dp", "seq", "task"),
            P("dp", None, ("task", "seq"), None),
            P("task", ("seq", "dp")),
            P("dp"),
        ),
        out_specs=(
            P("dp", "seq", "task"),
            P("dp", None, ("task", "seq"), None),
            P("task", ("seq", "dp")),
        ),
        check_vma=False,
    )
```

time: 328 us -> 264 us (0.80)
  the two profiles are of different devices: /device:TPU:8 before, /device:TPU:2 now
where the time goes in v1:
time: 264 us; the launch traced here: 263 us
  starting transfers between devices  88.8 us (34%)
  waiting for transfers between devices  62 us (23%)
  blocking collectives  41.2 us (16%)
  Pallas kernels  28.4 us (11%)
  local copies, waits for them, and re-layouts  16.9 us (6%)
  between operations  15 us (6%)
  matrix products  8.47 us (3%)
  other arithmetic  2.64 us (1%)
    all_to_all x1, blocking collectives, copy_for_each(): return lax.all_to_all(copies, axis, split_axis=0, concat_axis=0, tiled=True)  41.2 us
    ppermute x7, starting transfers between devices, compute(): piece = lax.ppermute(piece, 'dp', ring)  29.4 us
    ppermute x1, waiting for transfers between devices, compute(): came = lax.ppermute(theirs.astype(jnp.bfloat16), 'task', far_swap)  24.6 us
    pallas_call x1, Pallas kernels, grads_of(): pl.pallas_call(grads_kernel, grid=(n // tile,), in_specs=[pl.BlockSpec((n...  17.3 us
    ppermute x3, starting transfers between devices, compute(): shares.append(lax.ppermute(sums, 'task', pairs))  16.4 us
    pallas_call x1, Pallas kernels, probs_of(): pl.pallas_call(probs_kernel, grid=(n // tile,), in_specs=[pl.BlockSpec(me...  11.1 us
    ppermute x1, waiting for transfers between devices, compute(): across = lax.ppermute(resid, 'task', far_swap)  10.8 us
    all_to_all x1, waiting for transfers between devices, compute(): lax.all_to_all(resid_full, 'seq', split_axis=1, concat_axis=0, tiled=True)  9.06 us
  transfers between devices with their start and end apart: 19, of which 8 were waited for; matrix products, arithmetic and copies ran while one was open for 9% of the time, Pallas kernels for 4%

profile of v1, /device:TPU:2, one launch (start us, length us, event | category | flops | bytes accessed | tf_op | source)
XLA Modules:
  0.0 263.4 jit_solution(12036892530602397623)
XLA Ops:
  8.1 41.2 %all_to_all.48 = bf16[8,32,1024]{2,1,0:T(8,128)(2,1)} all-to-all(bf16[8,32,1024]{2,1,0:T(8,128)(2,1)S(1)} %broadcast_in_dim.21), channel_id=1, replica_groups=mesh['task'=4,'seq'=16,'dp'=8] {'dp'}, dimensions={0} | all-to-all | bytes 1048576 | tf_op jit(solution)/shard_map/all_to_all | solution.py:127
  51.0 2.5 broadcast_in_dim.22
  53.5 7.5 %all-to-all-start.1 = ((bf16[16,128,1024]{2,1,0:T(8,128)(2,1)}), bf16[16,128,1024]{2,1,0:T(8,128)(2,1)}, u32[]{:S(2)}, u32[]{:S(2)}) async-start(bf16[16,128,1024]{2,1,0:T(8,128)(2,1)} %broadcast_in_dim.22), calls=%async_computation.1 | async-start | bytes 8388608 | tf_op jit(solution)/shard_map/all_to_all | solution.py:127
  61.0 1.9 collective-permute-start
  65.0 8.2 %collective-permute-start.1 = (bf16[128,1024]{0,1:T(8,128)(2,1)S(1)}, bf16[128,1024]{0,1:T(8,128)(2,1)S(1)}, u32[]{:S(2)}, u32[]{:S(2)}) collective-permute-start(bf16[128,1024]{0,1:T(8,128)(2,1)S(1)} %fusion.11), channel_id=1, source_target_pairs={{0,256},{256,0},{128,384},{384,128},{1,257},{257,1},{129,385},{385... | collective-permute-start | bytes 786440 | tf_op jit(solution)/shard_map/ppermute | solution.py:159
  74.2 24.6 %collective-permute-done.1 = bf16[128,1024]{0,1:T(8,128)(2,1)S(1)} collective-permute-done((bf16[128,1024]{0,1:T(8,128)(2,1)S(1)}, bf16[128,1024]{0,1:T(8,128)(2,1)S(1)}, u32[]{:S(2)}, u32[]{:S(2)}) %collective-permute-start.1) | collective-permute-done | bytes 262176 | tf_op jit(solution)/shard_map/ppermute | solution.py:159
  99.0 2.1 collective-permute-start.2
  101.1 6.3 %collective-permute-start.3 = (f32[1,256]{1,0:T(1,128)S(1)}, f32[1,256]{1,0:T(1,128)S(1)}, u32[]{:S(2)}, u32[]{:S(2)}) collective-permute-start(f32[1,256]{1,0:T(1,128)S(1)} %bitcast.122), channel_id=1, source_target_pairs={{0,256},{256,0},{128,384},{384,128},{1,257},{257,1},{129,385},{385... | collective-permute-start | bytes 3080 | tf_op jit(solution)/shard_map/ppermute | solution.py:175
  107.4 8.1 %collective-permute-start.4 = (f32[1,256]{1,0:T(1,128)S(1)}, f32[1,256]{1,0:T(1,128)S(1)}, u32[]{:S(2)}, u32[]{:S(2)}) collective-permute-start(f32[1,256]{1,0:T(1,128)S(1)} %bitcast.123), channel_id=1, source_target_pairs={{0,384},{384,0},{128,256},{256,128},{1,385},{385,1},{129,257},{257... | collective-permute-start | bytes 3080 | tf_op jit(solution)/shard_map/ppermute | solution.py:175
  115.5 5.5 %collective-permute-done.4 = f32[1,256]{1,0:T(1,128)S(1)} collective-permute-done((f32[1,256]{1,0:T(1,128)S(1)}, f32[1,256]{1,0:T(1,128)S(1)}, u32[]{:S(2)}, u32[]{:S(2)}) %collective-permute-start.4) | collective-permute-done | bytes 1056 | tf_op jit(solution)/shard_map/ppermute | solution.py:175
  121.2 8.3 %collective-permute-start.6 = (bf16[128,1024]{0,1:T(8,128)(2,1)S(1)}, bf16[128,1024]{0,1:T(8,128)(2,1)S(1)}, u32[]{:S(2)}, u32[]{:S(2)}) collective-permute-start(bf16[128,1024]{0,1:T(8,128)(2,1)S(1)} %fusion.7), channel_id=1, source_target_pairs={{0,256},{256,0},{128,384},{384,128},{1,257},{257,1},{129,385},{385... | collective-permute-start | bytes 786440 | tf_op jit(solution)/shard_map/ppermute | solution.py:183
  129.5 1.9 collective-permute-start.5
  131.4 10.8 %collective-permute-done.6 = bf16[128,1024]{0,1:T(8,128)(2,1)S(1)} collective-permute-done((bf16[128,1024]{0,1:T(8,128)(2,1)S(1)}, bf16[128,1024]{0,1:T(8,128)(2,1)S(1)}, u32[]{:S(2)}, u32[]{:S(2)}) %collective-permute-start.6) | collective-permute-done | bytes 262176 | tf_op jit(solution)/shard_map/ppermute | solution.py:183
  142.3 1.9 collective-permute-start.7
  146.8 7.2 %all-to-all-start.2 = ((bf16[128,16,256]{0,2,1:T(8,128)(2,1)}), bf16[128,16,256]{0,2,1:T(8,128)(2,1)S(1)}, u32[]{:S(2)}, u32[]{:S(2)}) async-start(bf16[128,16,256]{0,2,1:T(8,128)(2,1)} %bitcast.19), calls=%async_computation.2 | async-start | bytes 2097152 | tf_op jit(solution)/shard_map/all_to_all | solution.py:200
  158.6 11.1 %probs.1.p_ref = bf16[2048,2048]{1,0:T(8,128)(2,1)} custom-call(s32[1]{0:T(128)S(6)} %copy.37.length_ref, bf16[2048,64]{1,0:T(8,128)(2,1)} %copy.24.q_ref, bf16[2048,64]{1,0:T(8,128)(2,1)} %copy.25.k_ref), custom_call_target="tpu_custom_call" | custom-call | flops 2147483648 | bytes 8388608 | tf_op jit(solution)/shard_map/probs/pallas_call | solution.py:45
  170.6 9.1 %all-to-all-done.2 = bf16[128,16,256]{0,2,1:T(8,128)(2,1)S(1)} async-done(((bf16[128,16,256]{0,2,1:T(8,128)(2,1)}), bf16[128,16,256]{0,2,1:T(8,128)(2,1)S(1)}, u32[]{:S(2)}, u32[]{:S(2)}) %all-to-all-start.2) | async-done | bytes 1048608 | tf_op jit(solution)/shard_map/all_to_all | solution.py:200
  179.8 3.5 %fusion.24 = (bf16[8,32,1024]{2,1,0:T(8,128)(2,1)S(1)}, f32[8,32,1024]{2,1,0:T(8,128)S(1)}) fusion(bf16[8,32,2048]{2,1,0:T(8,128)(2,1)S(1)} %bitcast.117, bf16[2048,1024]{1,0:T(8,128)(2,1)} %bitcast.18), kind=kOutput, calls=%fused_computation.57 | convolution fusion | flops 1074003968 | bytes 6815744 | tf_op jit(solution)/shard_map/dot_general | solution.py:201
  183.3 1.9 collective-permute-start.10
  185.2 11.2 %collective-permute-start.11 = (bf16[32,1024]{1,0:T(8,128)(2,1)S(1)}, bf16[32,1024]{1,0:T(8,128)(2,1)S(1)}, u32[]{:S(2)}, u32[]{:S(2)}) collective-permute-start(bf16[32,1024]{1,0:T(8,128)(2,1)S(1)} %get-tuple-element.33), channel_id=1, source_target_pairs={{0,4},{1,5},{2,6},{3,7},{4,0},{5,1},{6,2},{7,3},{8,12},{9,13},{10,... | collective-permute-start | bytes 196616 | tf_op jit(solution)/shard_map/ppermute | solution.py:211
  196.5 1.9 collective-permute-start.12
  198.4 7.2 %collective-permute-start.13 = (bf16[32,1024]{1,0:T(8,128)(2,1)S(1)}, bf16[32,1024]{1,0:T(8,128)(2,1)S(1)}, u32[]{:S(2)}, u32[]{:S(2)}) collective-permute-start(bf16[32,1024]{1,0:T(8,128)(2,1)S(1)} %get-tuple-element.31), channel_id=1, source_target_pairs={{0,6},{1,7},{2,0},{3,1},{4,2},{5,3},{6,4},{7,5},{8,14},{9,15},{10,... | collective-permute-start | bytes 196616 | tf_op jit(solution)/shard_map/ppermute | solution.py:211
  205.6 2.5 collective-permute-start.14
  208.1 5.0 %convolution_convert_fusion = bf16[128,1024]{1,0:T(8,128)(2,1)S(1)} fusion(bf16[128,4096]{0,1:T(8,128)(2,1)} %pad_maximum_fusion, bf16[4096,1024]{1,0:T(8,128)(2,1)} %all-gather.2.cloned.1.call-done), kind=kOutput, calls=%fused_computation.2 | convolution fusion | flops 1073872896 | bytes 9699328 | tf_op jit(solution)/shard_map/dot_general | solution.py:215
  214.0 6.1 %all-to-all-start.3 = ((bf16[128,16,64]{0,2,1:T(8,128)(2,1)}), bf16[128,16,64]{0,2,1:T(8,128)(2,1)S(1)}, u32[]{:S(2)}, u32[]{:S(2)}) async-start(bf16[128,16,64]{0,2,1:T(8,128)(2,1)} %bitcast.21), calls=%async_computation.3 | async-start | bytes 524288 | tf_op jit(solution)/shard_map/all_to_all | solution.py:219
  220.1 2.7 %collective-permute-start.8 = (bf16[32,1024]{1,0:T(8,128)(2,1)S(1)}, bf16[32,1024]{1,0:T(8,128)(2,1)S(1)}, u32[]{:S(2)}, u32[]{:S(2)}) collective-permute-start(bf16[32,1024]{1,0:T(8,128)(2,1)S(1)} %get-tuple-element.29), channel_id=1, source_target_pairs={{0,1},{1,2},{2,3},{3,4},{4,5},{5,6},{6,7},{7,0},{8,9},{9,10},{10,1... | collective-permute-start | bytes 196616 | tf_op jit(solution)/shard_map/ppermute | solution.py:211
  222.8 1.9 collective-permute-start.9
  224.7 2.1 constant_dynamic-slice_fusion.o_ref
  226.8 6.1 %collective-permute-done.8 = bf16[32,1024]{1,0:T(8,128)(2,1)S(1)} collective-permute-done((bf16[32,1024]{1,0:T(8,128)(2,1)S(1)}, bf16[32,1024]{1,0:T(8,128)(2,1)S(1)}, u32[]{:S(2)}, u32[]{:S(2)}) %collective-permute-start.8) | collective-permute-done | bytes 65568 | tf_op jit(solution)/shard_map/ppermute | solution.py:211
  232.8 2.5 collective-permute-done.9
  237.1 17.3 %grads.1 = bf16[2048,192]{1,0:T(8,128)(2,1)} custom-call(bf16[2048,2048]{1,0:T(8,128)(2,1)} %probs.1.p_ref, bf16[2048,64]{1,0:T(8,128)(2,1)} %copy.24.q_ref, bf16[2048,64]{1,0:T(8,128)(2,1)} %bitcast.114, bf16[2048,64]{1,0:T(8,128)(2,1)} %constant_dynamic-slice_fusion.o_ref, bf16[2048,64]{1,0:T(8,128)(2,1)} %copy.25.k_ref, bf16[2048,64]{1,0:T(8,128)(2,1)} %copy.31.v_ref, ...), custom_call_target="tpu_custom_call" | custom-call | flops 2147483648 | bytes 8388608 | tf_op jit(solution)/shard_map/grads/pallas_call | solution.py:103
  254.4 2.2 copy.33
  (46 shorter events, 16.3 us)
Async XLA Ops:
  7.2 43.8 %copy-start.1 = (bf16[1,128,1024]{2,1,0:T(8,128)(2,1)S(1)}, bf16[1,128,1024]{2,1,0:T(8,128)(2,1)}, u32[]{:S(2)}) copy-start(bf16[1,128,1024]{2,1,0:T(8,128)(2,1)} %param.10) | copy-start | bytes 786436
  7.2 200.9 %all-gather.2.cloned.1.call-start = ((), (), s32[]{:S(2)}) async-start(), calls=%async_computation.4 | async-start | bytes 8912896 | tf_op jit(solution)/shard_map/all_gather | solution.py:165
  53.5 93.4 %all-to-all-start.1 = ((bf16[16,128,1024]{2,1,0:T(8,128)(2,1)}), bf16[16,128,1024]{2,1,0:T(8,128)(2,1)}, u32[]{:S(2)}, u32[]{:S(2)}) async-start(bf16[16,128,1024]{2,1,0:T(8,128)(2,1)} %broadcast_in_dim.22), calls=%async_computation.1 | async-start | bytes 8388608 | tf_op jit(solution)/shard_map/all_to_all | solution.py:127
  60.9 12.3 %copy-start.2 = (bf16[1,128,1024]{2,1,0:T(8,128)(2,1)S(1)}, bf16[1,128,1024]{2,1,0:T(8,128)(2,1)}, u32[]{:S(2)}) copy-start(bf16[1,128,1024]{2,1,0:T(8,128)(2,1)} %param.8) | copy-start | bytes 786436
  61.0 3.8 %collective-permute-start = (bf16[128,2,1024]{0,2,1:T(8,128)(2,1)S(1)}, bf16[128,2,1024]{0,2,1:T(8,128)(2,1)S(1)}, u32[]{:S(2)}, u32[]{:S(2)}) collective-permute-start(bf16[128,2,1024]{0,2,1:T(8,128)(2,1)S(1)} %fusion.8), channel_id=1, source_target_pairs={{0,128},{128,0},{256,384},{384,256},{1,129},{129,1},{257,385},{385... | collective-permute-start | bytes 1572872 | tf_op jit(solution)/shard_map/ppermute | solution.py:155
  65.0 33.7 %collective-permute-start.1 = (bf16[128,1024]{0,1:T(8,128)(2,1)S(1)}, bf16[128,1024]{0,1:T(8,128)(2,1)S(1)}, u32[]{:S(2)}, u32[]{:S(2)}) collective-permute-start(bf16[128,1024]{0,1:T(8,128)(2,1)S(1)} %fusion.11), channel_id=1, source_target_pairs={{0,256},{256,0},{128,384},{384,128},{1,257},{257,1},{129,385},{385... | collective-permute-start | bytes 786440 | tf_op jit(solution)/shard_map/ppermute | solution.py:159
  99.0 55.1 %copy-start = (bf16[1,2048,1,192]{1,3,2,0:T(8,128)(2,1)S(1)}, bf16[1,2048,1,192]{1,3,2,0:T(8,128)(2,1)}, u32[]{:S(2)}) copy-start(bf16[1,2048,1,192]{1,3,2,0:T(8,128)(2,1)} %param.11) | copy-start | bytes 2359300
  99.0 16.5 %collective-permute-start.2 = (f32[1,256]{1,0:T(1,128)S(1)}, f32[1,256]{1,0:T(1,128)S(1)}, u32[]{:S(2)}, u32[]{:S(2)}) collective-permute-start(f32[1,256]{1,0:T(1,128)S(1)} %bitcast.121), channel_id=1, source_target_pairs={{0,128},{128,0},{256,384},{384,256},{1,129},{129,1},{257,385},{385... | collective-permute-start | bytes 3080 | tf_op jit(solution)/shard_map/ppermute | solution.py:175
  101.1 14.4 %collective-permute-start.3 = (f32[1,256]{1,0:T(1,128)S(1)}, f32[1,256]{1,0:T(1,128)S(1)}, u32[]{:S(2)}, u32[]{:S(2)}) collective-permute-start(f32[1,256]{1,0:T(1,128)S(1)} %bitcast.122), channel_id=1, source_target_pairs={{0,256},{256,0},{128,384},{384,128},{1,257},{257,1},{129,385},{385... | collective-permute-start | bytes 3080 | tf_op jit(solution)/shard_map/ppermute | solution.py:175
  107.4 13.6 %collective-permute-start.4 = (f32[1,256]{1,0:T(1,128)S(1)}, f32[1,256]{1,0:T(1,128)S(1)}, u32[]{:S(2)}, u32[]{:S(2)}) collective-permute-start(f32[1,256]{1,0:T(1,128)S(1)} %bitcast.123), channel_id=1, source_target_pairs={{0,384},{384,0},{128,256},{256,128},{1,385},{385,1},{129,257},{257... | collective-permute-start | bytes 3080 | tf_op jit(solution)/shard_map/ppermute | solution.py:175
  121.2 21.0 %collective-permute-start.6 = (bf16[128,1024]{0,1:T(8,128)(2,1)S(1)}, bf16[128,1024]{0,1:T(8,128)(2,1)S(1)}, u32[]{:S(2)}, u32[]{:S(2)}) collective-permute-start(bf16[128,1024]{0,1:T(8,128)(2,1)S(1)} %fusion.7), channel_id=1, source_target_pairs={{0,256},{256,0},{128,384},{384,128},{1,257},{257,1},{129,385},{385... | collective-permute-start | bytes 786440 | tf_op jit(solution)/shard_map/ppermute | solution.py:183
  129.5 14.7 %collective-permute-start.5 = (bf16[128,1024]{0,1:T(8,128)(2,1)S(1)}, bf16[128,1024]{0,1:T(8,128)(2,1)S(1)}, u32[]{:S(2)}, u32[]{:S(2)}) collective-permute-start(bf16[128,1024]{0,1:T(8,128)(2,1)S(1)} %fusion.7), channel_id=1, source_target_pairs={{0,128},{128,0},{256,384},{384,256},{1,129},{129,1},{257,385},{385... | collective-permute-start | bytes 786440 | tf_op jit(solution)/shard_map/ppermute | solution.py:182
  142.3 3.4 %collective-permute-start.7 = (bf16[128,1024]{0,1:T(8,128)(2,1)S(1)}, bf16[128,1024]{0,1:T(8,128)(2,1)S(1)}, u32[]{:S(2)}, u32[]{:S(2)}) collective-permute-start(bf16[128,1024]{0,1:T(8,128)(2,1)S(1)} %collective-permute-done.6), channel_id=1, source_target_pairs={{0,128},{128,0},{256,384},{384,256},{1,129},{129,1},{257,385},{385... | collective-permute-start | bytes 786440 | tf_op jit(solution)/shard_map/ppermute | solution.py:184
  146.8 32.8 %all-to-all-start.2 = ((bf16[128,16,256]{0,2,1:T(8,128)(2,1)}), bf16[128,16,256]{0,2,1:T(8,128)(2,1)S(1)}, u32[]{:S(2)}, u32[]{:S(2)}) async-start(bf16[128,16,256]{0,2,1:T(8,128)(2,1)} %bitcast.19), calls=%async_computation.2 | async-start | bytes 2097152 | tf_op jit(solution)/shard_map/all_to_all | solution.py:200
  183.3 36.7 %collective-permute-start.10 = (bf16[32,1024]{1,0:T(8,128)(2,1)S(1)}, bf16[32,1024]{1,0:T(8,128)(2,1)S(1)}, u32[]{:S(2)}, u32[]{:S(2)}) collective-permute-start(bf16[32,1024]{1,0:T(8,128)(2,1)S(1)} %get-tuple-element.34), channel_id=1, source_target_pairs={{0,3},{1,4},{2,5},{3,6},{4,7},{5,0},{6,1},{7,2},{8,11},{9,12},{10,... | collective-permute-start | bytes 196616 | tf_op jit(solution)/shard_map/ppermute | solution.py:211
  185.2 37.5 %collective-permute-start.11 = (bf16[32,1024]{1,0:T(8,128)(2,1)S(1)}, bf16[32,1024]{1,0:T(8,128)(2,1)S(1)}, u32[]{:S(2)}, u32[]{:S(2)}) collective-permute-start(bf16[32,1024]{1,0:T(8,128)(2,1)S(1)} %get-tuple-element.33), channel_id=1, source_target_pairs={{0,4},{1,5},{2,6},{3,7},{4,0},{5,1},{6,2},{7,3},{8,12},{9,13},{10,... | collective-permute-start | bytes 196616 | tf_op jit(solution)/shard_map/ppermute | solution.py:211
  196.5 30.3 %collective-permute-start.12 = (bf16[32,1024]{1,0:T(8,128)(2,1)S(1)}, bf16[32,1024]{1,0:T(8,128)(2,1)S(1)}, u32[]{:S(2)}, u32[]{:S(2)}) collective-permute-start(bf16[32,1024]{1,0:T(8,128)(2,1)S(1)} %get-tuple-element.32), channel_id=1, source_target_pairs={{0,5},{1,6},{2,7},{3,0},{4,1},{5,2},{6,3},{7,4},{8,13},{9,14},{10,... | collective-permute-start | bytes 196616 | tf_op jit(solution)/shard_map/ppermute | solution.py:211
  198.4 28.3 %collective-permute-start.13 = (bf16[32,1024]{1,0:T(8,128)(2,1)S(1)}, bf16[32,1024]{1,0:T(8,128)(2,1)S(1)}, u32[]{:S(2)}, u32[]{:S(2)}) collective-permute-start(bf16[32,1024]{1,0:T(8,128)(2,1)S(1)} %get-tuple-element.31), channel_id=1, source_target_pairs={{0,6},{1,7},{2,0},{3,1},{4,2},{5,3},{6,4},{7,5},{8,14},{9,15},{10,... | collective-permute-start | bytes 196616 | tf_op jit(solution)/shard_map/ppermute | solution.py:211
  205.6 21.2 %collective-permute-start.14 = (bf16[32,1024]{1,0:T(8,128)(2,1)S(1)}, bf16[32,1024]{1,0:T(8,128)(2,1)S(1)}, u32[]{:S(2)}, u32[]{:S(2)}) collective-permute-start(bf16[32,1024]{1,0:T(8,128)(2,1)S(1)} %get-tuple-element.30), channel_id=1, source_target_pairs={{0,7},{1,0},{2,1},{3,2},{4,3},{5,4},{6,5},{7,6},{8,15},{9,8},{10,9... | collective-permute-start | bytes 196616 | tf_op jit(solution)/shard_map/ppermute | solution.py:211
  214.0 22.1 %all-to-all-start.3 = ((bf16[128,16,64]{0,2,1:T(8,128)(2,1)}), bf16[128,16,64]{0,2,1:T(8,128)(2,1)S(1)}, u32[]{:S(2)}, u32[]{:S(2)}) async-start(bf16[128,16,64]{0,2,1:T(8,128)(2,1)} %bitcast.21), calls=%async_computation.3 | async-start | bytes 524288 | tf_op jit(solution)/shard_map/all_to_all | solution.py:219
  220.1 12.8 %collective-permute-start.8 = (bf16[32,1024]{1,0:T(8,128)(2,1)S(1)}, bf16[32,1024]{1,0:T(8,128)(2,1)S(1)}, u32[]{:S(2)}, u32[]{:S(2)}) collective-permute-start(bf16[32,1024]{1,0:T(8,128)(2,1)S(1)} %get-tuple-element.29), channel_id=1, source_target_pairs={{0,1},{1,2},{2,3},{3,4},{4,5},{5,6},{6,7},{7,0},{8,9},{9,10},{10,1... | collective-permute-start | bytes 196616 | tf_op jit(solution)/shard_map/ppermute | solution.py:211
  222.8 12.6 %collective-permute-start.9 = (bf16[32,1024]{1,0:T(8,128)(2,1)S(1)}, bf16[32,1024]{1,0:T(8,128)(2,1)S(1)}, u32[]{:S(2)}, u32[]{:S(2)}) collective-permute-start(bf16[32,1024]{1,0:T(8,128)(2,1)S(1)} %get-tuple-element.35), channel_id=1, source_target_pairs={{0,2},{1,3},{2,4},{3,5},{4,6},{5,7},{6,0},{7,1},{8,10},{9,11},{10,... | collective-permute-start | bytes 196616 | tf_op jit(solution)/shard_map/ppermute | solution.py:211
Sparse Core Ops, SparseCore 0:
  49.5 129.1 all-gather.1

commit v2 on v1

--- a/solution.py
+++ b/solution.py
@@ -9,7 +9,6 @@
 eps_norm = 1e-06
 core_swap = [(0, 1), (1, 0), (2, 3), (3, 2)]
 far_swap = [(0, 2), (2, 0), (1, 3), (3, 1)]
-corner_swap = [(0, 3), (3, 0), (1, 2), (2, 1)]
 NT = (((1,), (1,)), ((), ()))
 NN = (((1,), (0,)), ((), ()))
 tile = 256
@@ -127,10 +126,6 @@
     return lax.all_to_all(copies, axis, split_axis=0, concat_axis=0, tiled=True)
 
 
-def pick(stack, index):
-    return lax.dynamic_index_in_dim(stack, index, 0, keepdims=False)
-
-
 def compute(enc_grads, hidden, final_gain, attn_out, qkv, out_weight, doc_lengths):
     rows, feature_cols = enc_grads.shape[2:]
     tasks = lax.axis_size("task")
@@ -141,14 +136,24 @@
     seq_len = qkv.shape[1]
     head_size = qkv.shape[3] // 3
 
+    dp_pos = lax.axis_index("dp")
+    slab = out_weight.T[None, None, None]
+    for axis, bit in ((0, 4), (1, 2), (2, 1)):
+        other = lax.ppermute(slab, "dp", [(d, d ^ bit) for d in range(dp_count)])
+        lower = (dp_pos & bit) == 0
+        slab = jnp.concatenate(
+            [jnp.where(lower, slab, other), jnp.where(lower, other, slab)], axis=axis
+        )
+    slab = slab.reshape(-1, slab.shape[-1])
+    weight = lax.all_gather(slab, "seq", axis=0, tiled=True)
+
     heads = qkv.reshape(seq_len, 3 * head_size)
     query = heads[:, :head_size]
     key_rows = heads[:, head_size : 2 * head_size]
     value_rows = heads[:, 2 * head_size :]
-    probs = probs_of(doc_lengths, query, key_rows)
-
-    slab = copy_for_each(out_weight.T, "dp")
-    slab = slab.reshape(-1, slab.shape[-1])
+    query_after, slab = lax.optimization_barrier((query, slab))
+    probs = probs_of(doc_lengths, query_after, key_rows)
+
     terms = enc_grads[0, 0].reshape(rows, 2, 2, share_cols)
     kept = jnp.where(core == 0, terms[:, :, 0], terms[:, :, 1])
     given = jnp.where(core == 0, terms[:, :, 1], terms[:, :, 0])
@@ -159,10 +164,8 @@
     came = lax.ppermute(theirs.astype(jnp.bfloat16), "task", far_swap)
     summed = mine + came.astype(jnp.float32)
 
-    saved_tok, slab = lax.optimization_barrier((attn_out[0], slab))
-    saved_all = copy_for_each(saved_tok, "seq")
+    saved_all = copy_for_each(attn_out[0], "seq")
     saved_all = saved_all.reshape(seq_len, -1)
-    weight = lax.all_gather(slab, "seq", axis=0, tiled=True)
 
     stream = hidden[0].astype(jnp.float32)
     gain = lax.dynamic_slice_in_dim(final_gain, task_pos * share_cols, share_cols, 0)
@@ -170,10 +173,8 @@
         [jnp.sum(stream * stream, axis=-1), jnp.sum(gain * summed * stream, axis=-1)]
     )
     sums = sums[None]
-    shares = [sums]
-    for pairs in (core_swap, far_swap, corner_swap):
-        shares.append(lax.ppermute(sums, "task", pairs))
-    sums = (shares[0] + shares[1] + shares[2] + shares[3])[0]
+    sums = sums + lax.ppermute(sums, "task", core_swap)
+    sums = (sums + lax.ppermute(sums, "task", far_swap))[0]
     squares, cross_sum = sums[:rows], sums[rows:]
     scale_inv = lax.rsqrt(squares / feature_cols + eps_norm)[:, None]
     cross_mean = cross_sum[:, None] * scale_inv / feature_cols
@@ -201,16 +202,16 @@
     grad_block = lax.dot_general(
         resid_cols, saved_all, (((0,), (0,)), ((), ())), preferred_element_type=jnp.float32
     )
-    blocks = grad_block.reshape(dp_count, -1, grad_block.shape[-1])
-    sent = blocks.astype(jnp.bfloat16)
-    dp_pos = lax.axis_index("dp")
-    weight_sum = pick(blocks, dp_pos)
-    for step in range(1, dp_count):
-        ring = [(d, (d + step) % dp_count) for d in range(dp_count)]
-        piece = pick(sent, (dp_pos + step) % dp_count)
-        piece = lax.ppermute(piece, "dp", ring)
-        weight_sum = weight_sum + piece.astype(jnp.float32)
-    weight_grad = weight_sum.T
+    total = grad_block.reshape(2, 2, 2, -1, grad_block.shape[-1])
+    for axis, bit in ((2, 1), (1, 2), (0, 4)):
+        lower = (dp_pos & bit) == 0
+        first, second = (
+            lax.index_in_dim(total, side, axis, keepdims=True) for side in (0, 1)
+        )
+        given = jnp.where(lower, second, first).astype(jnp.bfloat16)
+        came = lax.ppermute(given, "dp", [(d, d ^ bit) for d in range(dp_count)])
+        total = jnp.where(lower, first, second) + came.astype(jnp.float32)
+    weight_grad = total.reshape(total.shape[-2:]).T
 
     head_grad = lax.dot_general(
         resid_full, weight, NN, preferred_element_type=jnp.float32

time: 264 us -> 264 us (level)
  the two profiles are of different devices: /device:TPU:2 before, /device:TPU:32 now
where the time goes in v2:
time: 264 us; the launch traced here: 263 us
  starting transfers between devices  106 us (40%)
  waiting for transfers between devices  84.6 us (32%)
  Pallas kernels  28.3 us (11%)
  local copies, waits for them, and re-layouts  16 us (6%)
  between operations  15.1 us (6%)
  matrix products  8.62 us (3%)
  other arithmetic  4.62 us (2%)
    all_to_all x1, waiting for transfers between devices, compute(): lax.all_to_all(resid_full, 'seq', split_axis=1, concat_axis=0, tiled=True)  25.7 us
    ppermute x1, waiting for transfers between devices, compute(): came = lax.ppermute(theirs.astype(jnp.bfloat16), 'task', far_swap)  22.6 us
    ppermute x3, starting transfers between devices, compute(): came = lax.ppermute(given, 'dp', [(d, d ^ bit) for d in range(dp_count)])  21.2 us
    ppermute x3, starting transfers between devices, compute(): other = lax.ppermute(slab, 'dp', [(d, d ^ bit) for d in range(dp_count)])  17.5 us
    pallas_call x1, Pallas kernels, grads_of(): pl.pallas_call(grads_kernel, grid=(n // tile,), in_specs=[pl.BlockSpec((n...  17.3 us
    ppermute x3, waiting for transfers between devices, compute(): other = lax.ppermute(slab, 'dp', [(d, d ^ bit) for d in range(dp_count)])  15.9 us
    ppermute x1, starting transfers between devices, compute(): came = lax.ppermute(theirs.astype(jnp.bfloat16), 'task', far_swap)  14.7 us
    ppermute x1, starting transfers between devices, compute(): across = lax.ppermute(resid, 'task', far_swap)  11.5 us
  transfers between devices with their start and end apart: 17, of which 12 were waited for; matrix products, arithmetic and copies ran while one was open for 9% of the time, Pallas kernels for 4%

profile of v2, /device:TPU:32, one launch (start us, length us, event | category | flops | bytes accessed | tf_op | source)
XLA Modules:
  0.0 263.2 jit_solution(6329312857145775961)
XLA Ops:
  7.2 9.2 %collective-permute-start.4 = (bf16[1,1,1,32,1024]{4,3,2,1,0:T(8,128)(2,1)}, bf16[1,1,1,32,1024]{4,3,2,1,0:T(8,128)(2,1)S(1)}, u32[]{:S(2)}, u32[]{:S(2)}) collective-permute-start(bf16[1,1,1,32,1024]{4,3,2,1,0:T(8,128)(2,1)} %bitcast.96), channel_id=1, source_target_pairs={{0,4},{1,5},{2,6},{3,7},{4,0},{5,1},{6,2},{7,3},{8,12},{9,13},{10,... | collective-permute-start | bytes 196616 | tf_op jit(solution)/shard_map/ppermute | solution.py:142
  16.5 5.3 %collective-permute-done.4 = bf16[1,1,1,32,1024]{4,3,2,1,0:T(8,128)(2,1)S(1)} collective-permute-done((bf16[1,1,1,32,1024]{4,3,2,1,0:T(8,128)(2,1)}, bf16[1,1,1,32,1024]{4,3,2,1,0:T(8,128)(2,1)S(1)}, u32[]{:S(2)}, u32[]{:S(2)}) %collective-permute-start.4) | collective-permute-done | bytes 65568 | tf_op jit(solution)/shard_map/ppermute | solution.py:142
  22.7 4.3 %collective-permute-start.5 = (bf16[2,1,1,32,1024]{4,3,2,1,0:T(8,128)(2,1)S(1)}, bf16[2,1,1,32,1024]{4,3,2,1,0:T(8,128)(2,1)S(1)}, u32[]{:S(2)}, u32[]{:S(2)}) collective-permute-start(bf16[2,1,1,32,1024]{4,3,2,1,0:T(8,128)(2,1)S(1)} %pad_maximum_fusion.3), channel_id=1, source_target_pairs={{0,2},{1,3},{2,0},{3,1},{4,6},{5,7},{6,4},{7,5},{8,10},{9,11},{10,... | collective-permute-start | bytes 393224 | tf_op jit(solution)/shard_map/ppermute | solution.py:142
  27.0 4.4 %collective-permute-done.5 = bf16[2,1,1,32,1024]{4,3,2,1,0:T(8,128)(2,1)S(1)} collective-permute-done((bf16[2,1,1,32,1024]{4,3,2,1,0:T(8,128)(2,1)S(1)}, bf16[2,1,1,32,1024]{4,3,2,1,0:T(8,128)(2,1)S(1)}, u32[]{:S(2)}, u32[]{:S(2)}) %collective-permute-start.5) | collective-permute-done | bytes 131104 | tf_op jit(solution)/shard_map/ppermute | solution.py:142
  31.4 3.9 %collective-permute-start.6 = (bf16[2,2,1,32,1024]{4,3,2,1,0:T(8,128)(2,1)S(1)}, bf16[2,2,1,32,1024]{4,3,2,1,0:T(8,128)(2,1)S(1)}, u32[]{:S(2)}, u32[]{:S(2)}) collective-permute-start(bf16[2,2,1,32,1024]{4,3,2,1,0:T(8,128)(2,1)S(1)} %pad_maximum_fusion.2), channel_id=1, source_target_pairs={{0,1},{1,0},{2,3},{3,2},{4,5},{5,4},{6,7},{7,6},{8,9},{9,8},{10,11... | collective-permute-start | bytes 786440 | tf_op jit(solution)/shard_map/ppermute | solution.py:142
  35.4 6.2 %collective-permute-done.6 = bf16[2,2,1,32,1024]{4,3,2,1,0:T(8,128)(2,1)S(1)} collective-permute-done((bf16[2,2,1,32,1024]{4,3,2,1,0:T(8,128)(2,1)S(1)}, bf16[2,2,1,32,1024]{4,3,2,1,0:T(8,128)(2,1)S(1)}, u32[]{:S(2)}, u32[]{:S(2)}) %collective-permute-start.6) | collective-permute-done | bytes 262176 | tf_op jit(solution)/shard_map/ppermute | solution.py:142
  42.5 2.5 broadcast_in_dim.22
  45.0 7.2 %all-to-all-start = ((bf16[16,128,1024]{2,1,0:T(8,128)(2,1)}), bf16[16,128,1024]{2,1,0:T(8,128)(2,1)}, u32[]{:S(2)}, u32[]{:S(2)}) async-start(bf16[16,128,1024]{2,1,0:T(8,128)(2,1)} %broadcast_in_dim.22), calls=%async_computation | async-start | bytes 8388608 | tf_op jit(solution)/shard_map/all_to_all | solution.py:126
  53.0 1.9 collective-permute-start
  54.9 1.9 collective-permute-done
  57.0 14.7 %collective-permute-start.1 = (bf16[128,1024]{0,1:T(8,128)(2,1)S(1)}, bf16[128,1024]{0,1:T(8,128)(2,1)S(1)}, u32[]{:S(2)}, u32[]{:S(2)}) collective-permute-start(bf16[128,1024]{0,1:T(8,128)(2,1)S(1)} %fusion.11), channel_id=1, source_target_pairs={{0,256},{256,0},{128,384},{384,128},{1,257},{257,1},{129,385},{385... | collective-permute-start | bytes 786440 | tf_op jit(solution)/shard_map/ppermute | solution.py:164
  72.6 22.6 %collective-permute-done.1 = bf16[128,1024]{0,1:T(8,128)(2,1)S(1)} collective-permute-done((bf16[128,1024]{0,1:T(8,128)(2,1)S(1)}, bf16[128,1024]{0,1:T(8,128)(2,1)S(1)}, u32[]{:S(2)}, u32[]{:S(2)}) %collective-permute-start.1) | collective-permute-done | bytes 262176 | tf_op jit(solution)/shard_map/ppermute | solution.py:164
  95.5 1.9 collective-permute-start.2
  98.5 11.4 %collective-permute-start.3 = (f32[1,256]{1,0:T(1,128)S(1)}, f32[1,256]{1,0:T(1,128)S(1)}, u32[]{:S(2)}, u32[]{:S(2)}) collective-permute-start(f32[1,256]{1,0:T(1,128)S(1)} %add.50), channel_id=1, source_target_pairs={{0,256},{256,0},{128,384},{384,128},{1,257},{257,1},{129,385},{385... | collective-permute-start | bytes 3080 | tf_op jit(solution)/shard_map/ppermute | solution.py:177
  109.9 2.7 %collective-permute-done.3 = f32[1,256]{1,0:T(1,128)S(1)} collective-permute-done((f32[1,256]{1,0:T(1,128)S(1)}, f32[1,256]{1,0:T(1,128)S(1)}, u32[]{:S(2)}, u32[]{:S(2)}) %collective-permute-start.3) | collective-permute-done | bytes 1056 | tf_op jit(solution)/shard_map/ppermute | solution.py:177
  112.9 11.5 %collective-permute-start.8 = (bf16[128,1024]{0,1:T(8,128)(2,1)S(1)}, bf16[128,1024]{0,1:T(8,128)(2,1)S(1)}, u32[]{:S(2)}, u32[]{:S(2)}) collective-permute-start(bf16[128,1024]{0,1:T(8,128)(2,1)S(1)} %fusion.7), channel_id=1, source_target_pairs={{0,256},{256,0},{128,384},{384,128},{1,257},{257,1},{129,385},{385... | collective-permute-start | bytes 786440 | tf_op jit(solution)/shard_map/ppermute | solution.py:184
  124.5 1.9 collective-permute-start.7
  126.4 6.1 %collective-permute-done.8 = bf16[128,1024]{0,1:T(8,128)(2,1)S(1)} collective-permute-done((bf16[128,1024]{0,1:T(8,128)(2,1)S(1)}, bf16[128,1024]{0,1:T(8,128)(2,1)S(1)}, u32[]{:S(2)}, u32[]{:S(2)}) %collective-permute-start.8) | collective-permute-done | bytes 262176 | tf_op jit(solution)/shard_map/ppermute | solution.py:184
  132.5 1.9 collective-permute-start.9
  137.1 7.2 %all-to-all-start.1 = ((bf16[128,16,256]{0,2,1:T(8,128)(2,1)}), bf16[128,16,256]{0,2,1:T(8,128)(2,1)S(1)}, u32[]{:S(2)}, u32[]{:S(2)}) async-start(bf16[128,16,256]{0,2,1:T(8,128)(2,1)} %bitcast.21), calls=%async_computation.1 | async-start | bytes 2097152 | tf_op jit(solution)/shard_map/all_to_all | solution.py:201
  144.2 25.7 %all-to-all-done.1 = bf16[128,16,256]{0,2,1:T(8,128)(2,1)S(1)} async-done(((bf16[128,16,256]{0,2,1:T(8,128)(2,1)}), bf16[128,16,256]{0,2,1:T(8,128)(2,1)S(1)}, u32[]{:S(2)}, u32[]{:S(2)}) %all-to-all-start.1) | async-done | bytes 1048608 | tf_op jit(solution)/shard_map/all_to_all | solution.py:201
  170.1 3.6 %fusion = f32[2,2,2,32,1024]{4,3,2,1,0:T(8,128)S(1)} fusion(bf16[2,2,2,32,2048]{4,3,2,1,0:T(8,128)(2,1)S(1)} %bitcast.93, bf16[2048,1024]{1,0:T(8,128)(2,1)} %bitcast.20), kind=kOutput, calls=%fused_computation | convolution fusion | flops 1073741824 | bytes 6291456 | tf_op jit(solution)/shard_map/dot_general | solution.py:202
  173.8 1.9 collective-permute-start.10
  182.8 1.9 collective-permute-start.11
  184.7 11.1 %probs.1.p_ref = bf16[2048,2048]{1,0:T(8,128)(2,1)} custom-call(s32[1]{0:T(128)S(6)} %copy.38.length_ref, bf16[2048,64]{1,0:T(8,128)(2,1)} %copy.24.q_ref, bf16[2048,64]{1,0:T(8,128)(2,1)} %copy.25.k_ref), custom_call_target="tpu_custom_call" | custom-call | flops 2147483648 | bytes 8388608 | tf_op jit(solution)/shard_map/probs/pallas_call | solution.py:44
  196.7 17.3 %collective-permute-start.12 = (bf16[1,1,1,32,1024]{4,3,2,1,0:T(8,128)(2,1)S(1)}, bf16[1,1,1,32,1024]{4,3,2,1,0:T(8,128)(2,1)S(1)}, u32[]{:S(2)}, u32[]{:S(2)}) collective-permute-start(bf16[1,1,1,32,1024]{4,3,2,1,0:T(8,128)(2,1)S(1)} %select_convert_fusion.3), channel_id=1, source_target_pairs={{0,4},{1,5},{2,6},{3,7},{4,0},{5,1},{6,2},{7,3},{8,12},{9,13},{10,... | collective-permute-start | bytes 196616 | tf_op jit(solution)/shard_map/ppermute | solution.py:212
  214.1 5.0 %convolution_convert_fusion = bf16[128,1024]{1,0:T(8,128)(2,1)S(1)} fusion(bf16[128,4096]{0,1:T(8,128)(2,1)} %pad_maximum_fusion, bf16[4096,1024]{1,0:T(8,128)(2,1)} %all-gather.2.cloned.1.call-done), kind=kOutput, calls=%fused_computation.2 | convolution fusion | flops 1073872896 | bytes 9699328 | tf_op jit(solution)/shard_map/dot_general | solution.py:216
  219.9 7.5 %all-to-all-start.2 = ((bf16[128,16,64]{0,2,1:T(8,128)(2,1)}), bf16[128,16,64]{0,2,1:T(8,128)(2,1)S(1)}, u32[]{:S(2)}, u32[]{:S(2)}) async-start(bf16[128,16,64]{0,2,1:T(8,128)(2,1)} %bitcast.23), calls=%async_computation.2 | async-start | bytes 524288 | tf_op jit(solution)/shard_map/all_to_all | solution.py:220
  227.4 2.1 constant_dynamic-slice_fusion.o_ref
  230.1 5.7 %all-to-all-done.2 = bf16[128,16,64]{0,2,1:T(8,128)(2,1)S(1)} async-done(((bf16[128,16,64]{0,2,1:T(8,128)(2,1)}), bf16[128,16,64]{0,2,1:T(8,128)(2,1)S(1)}, u32[]{:S(2)}, u32[]{:S(2)}) %all-to-all-start.2) | async-done | bytes 262176 | tf_op jit(solution)/shard_map/all_to_all | solution.py:220
  236.9 17.3 %grads.1 = bf16[2048,192]{1,0:T(8,128)(2,1)} custom-call(bf16[2048,2048]{1,0:T(8,128)(2,1)} %probs.1.p_ref, bf16[2048,64]{1,0:T(8,128)(2,1)} %copy.29.q_ref, bf16[2048,64]{1,0:T(8,128)(2,1)} %bitcast.90, bf16[2048,64]{1,0:T(8,128)(2,1)} %constant_dynamic-slice_fusion.o_ref, bf16[2048,64]{1,0:T(8,128)(2,1)} %copy.25.k_ref, bf16[2048,64]{1,0:T(8,128)(2,1)} %copy.31.v_ref, ...), custom_call_target="tpu_custom_call" | custom-call | flops 2147483648 | bytes 8388608 | tf_op jit(solution)/shard_map/grads/pallas_call | solution.py:102
  254.1 2.2 copy.33
  (54 shorter events, 18.0 us)
Async XLA Ops:
  7.2 35.3 %copy-start.2 = (bf16[1,128,1024]{2,1,0:T(8,128)(2,1)S(1)}, bf16[1,128,1024]{2,1,0:T(8,128)(2,1)}, u32[]{:S(2)}) copy-start(bf16[1,128,1024]{2,1,0:T(8,128)(2,1)} %param.10) | copy-start | bytes 786436
  7.2 206.9 %all-gather.2.cloned.1.call-start = ((), (), s32[]{:S(2)}) async-start(), calls=%async_computation.3 | async-start | bytes 8912896 | tf_op jit(solution)/shard_map/all_gather | solution.py:148
  7.2 14.6 %collective-permute-start.4 = (bf16[1,1,1,32,1024]{4,3,2,1,0:T(8,128)(2,1)}, bf16[1,1,1,32,1024]{4,3,2,1,0:T(8,128)(2,1)S(1)}, u32[]{:S(2)}, u32[]{:S(2)}) collective-permute-start(bf16[1,1,1,32,1024]{4,3,2,1,0:T(8,128)(2,1)} %bitcast.96), channel_id=1, source_target_pairs={{0,4},{1,5},{2,6},{3,7},{4,0},{5,1},{6,2},{7,3},{8,12},{9,13},{10,... | collective-permute-start | bytes 196616 | tf_op jit(solution)/shard_map/ppermute | solution.py:142
  22.7 8.7 %collective-permute-start.5 = (bf16[2,1,1,32,1024]{4,3,2,1,0:T(8,128)(2,1)S(1)}, bf16[2,1,1,32,1024]{4,3,2,1,0:T(8,128)(2,1)S(1)}, u32[]{:S(2)}, u32[]{:S(2)}) collective-permute-start(bf16[2,1,1,32,1024]{4,3,2,1,0:T(8,128)(2,1)S(1)} %pad_maximum_fusion.3), channel_id=1, source_target_pairs={{0,2},{1,3},{2,0},{3,1},{4,6},{5,7},{6,4},{7,5},{8,10},{9,11},{10,... | collective-permute-start | bytes 393224 | tf_op jit(solution)/shard_map/ppermute | solution.py:142
  31.4 10.1 %collective-permute-start.6 = (bf16[2,2,1,32,1024]{4,3,2,1,0:T(8,128)(2,1)S(1)}, bf16[2,2,1,32,1024]{4,3,2,1,0:T(8,128)(2,1)S(1)}, u32[]{:S(2)}, u32[]{:S(2)}) collective-permute-start(bf16[2,2,1,32,1024]{4,3,2,1,0:T(8,128)(2,1)S(1)} %pad_maximum_fusion.2), channel_id=1, source_target_pairs={{0,1},{1,0},{2,3},{3,2},{4,5},{5,4},{6,7},{7,6},{8,9},{9,8},{10,11... | collective-permute-start | bytes 786440 | tf_op jit(solution)/shard_map/ppermute | solution.py:142
  45.0 7.3 %copy-start = (bf16[1,1,128,4096]{3,2,1,0:T(8,128)(2,1)S(1)}, bf16[1,1,128,4096]{3,2,1,0:T(8,128)(2,1)}, u32[]{:S(2)}) copy-start(bf16[1,1,128,4096]{3,2,1,0:T(8,128)(2,1)} %param.7) | copy-start | bytes 3145732
  45.0 92.0 %all-to-all-start = ((bf16[16,128,1024]{2,1,0:T(8,128)(2,1)}), bf16[16,128,1024]{2,1,0:T(8,128)(2,1)}, u32[]{:S(2)}, u32[]{:S(2)}) async-start(bf16[16,128,1024]{2,1,0:T(8,128)(2,1)} %broadcast_in_dim.22), calls=%async_computation | async-start | bytes 8388608 | tf_op jit(solution)/shard_map/all_to_all | solution.py:126
  52.2 19.5 %copy-start.3 = (bf16[1,128,1024]{2,1,0:T(8,128)(2,1)S(1)}, bf16[1,128,1024]{2,1,0:T(8,128)(2,1)}, u32[]{:S(2)}) copy-start(bf16[1,128,1024]{2,1,0:T(8,128)(2,1)} %param.8) | copy-start | bytes 786436
  53.0 3.8 %collective-permute-start = (bf16[128,2,1024]{0,2,1:T(8,128)(2,1)S(1)}, bf16[128,2,1024]{0,2,1:T(8,128)(2,1)S(1)}, u32[]{:S(2)}, u32[]{:S(2)}) collective-permute-start(bf16[128,2,1024]{0,2,1:T(8,128)(2,1)S(1)} %fusion.8), channel_id=1, source_target_pairs={{0,128},{128,0},{256,384},{384,256},{1,129},{129,1},{257,385},{385... | collective-permute-start | bytes 1572872 | tf_op jit(solution)/shard_map/ppermute | solution.py:160
  57.0 38.2 %collective-permute-start.1 = (bf16[128,1024]{0,1:T(8,128)(2,1)S(1)}, bf16[128,1024]{0,1:T(8,128)(2,1)S(1)}, u32[]{:S(2)}, u32[]{:S(2)}) collective-permute-start(bf16[128,1024]{0,1:T(8,128)(2,1)S(1)} %fusion.11), channel_id=1, source_target_pairs={{0,256},{256,0},{128,384},{384,128},{1,257},{257,1},{129,385},{385... | collective-permute-start | bytes 786440 | tf_op jit(solution)/shard_map/ppermute | solution.py:164
  95.5 3.1 %collective-permute-start.2 = (f32[1,256]{1,0:T(1,128)S(1)}, f32[1,256]{1,0:T(1,128)S(1)}, u32[]{:S(2)}, u32[]{:S(2)}) collective-permute-start(f32[1,256]{1,0:T(1,128)S(1)} %bitcast.97), channel_id=1, source_target_pairs={{0,128},{128,0},{256,384},{384,256},{1,129},{129,1},{257,385},{385... | collective-permute-start | bytes 3080 | tf_op jit(solution)/shard_map/ppermute | solution.py:176
  98.5 14.2 %collective-permute-start.3 = (f32[1,256]{1,0:T(1,128)S(1)}, f32[1,256]{1,0:T(1,128)S(1)}, u32[]{:S(2)}, u32[]{:S(2)}) collective-permute-start(f32[1,256]{1,0:T(1,128)S(1)} %add.50), channel_id=1, source_target_pairs={{0,256},{256,0},{128,384},{384,128},{1,257},{257,1},{129,385},{385... | collective-permute-start | bytes 3080 | tf_op jit(solution)/shard_map/ppermute | solution.py:177
  112.9 19.5 %collective-permute-start.8 = (bf16[128,1024]{0,1:T(8,128)(2,1)S(1)}, bf16[128,1024]{0,1:T(8,128)(2,1)S(1)}, u32[]{:S(2)}, u32[]{:S(2)}) collective-permute-start(bf16[128,1024]{0,1:T(8,128)(2,1)S(1)} %fusion.7), channel_id=1, source_target_pairs={{0,256},{256,0},{128,384},{384,128},{1,257},{257,1},{129,385},{385... | collective-permute-start | bytes 786440 | tf_op jit(solution)/shard_map/ppermute | solution.py:184
  124.5 9.9 %collective-permute-start.7 = (bf16[128,1024]{0,1:T(8,128)(2,1)S(1)}, bf16[128,1024]{0,1:T(8,128)(2,1)S(1)}, u32[]{:S(2)}, u32[]{:S(2)}) collective-permute-start(bf16[128,1024]{0,1:T(8,128)(2,1)S(1)} %fusion.7), channel_id=1, source_target_pairs={{0,128},{128,0},{256,384},{384,256},{1,129},{129,1},{257,385},{385... | collective-permute-start | bytes 786440 | tf_op jit(solution)/shard_map/ppermute | solution.py:183
  132.5 3.4 %collective-permute-start.9 = (bf16[128,1024]{0,1:T(8,128)(2,1)S(1)}, bf16[128,1024]{0,1:T(8,128)(2,1)S(1)}, u32[]{:S(2)}, u32[]{:S(2)}) collective-permute-start(bf16[128,1024]{0,1:T(8,128)(2,1)S(1)} %collective-permute-done.8), channel_id=1, source_target_pairs={{0,128},{128,0},{256,384},{384,256},{1,129},{129,1},{257,385},{385... | collective-permute-start | bytes 786440 | tf_op jit(solution)/shard_map/ppermute | solution.py:185
  137.1 32.9 %all-to-all-start.1 = ((bf16[128,16,256]{0,2,1:T(8,128)(2,1)}), bf16[128,16,256]{0,2,1:T(8,128)(2,1)S(1)}, u32[]{:S(2)}, u32[]{:S(2)}) async-start(bf16[128,16,256]{0,2,1:T(8,128)(2,1)} %bitcast.21), calls=%async_computation.1 | async-start | bytes 2097152 | tf_op jit(solution)/shard_map/all_to_all | solution.py:201
  170.1 5.6 %copy-start.1 = (bf16[1,2048,1,192]{1,3,2,0:T(8,128)(2,1)S(1)}, bf16[1,2048,1,192]{1,3,2,0:T(8,128)(2,1)}, u32[]{:S(2)}) copy-start(bf16[1,2048,1,192]{1,3,2,0:T(8,128)(2,1)} %param.11) | copy-start | bytes 2359300
  173.8 8.8 %collective-permute-start.10 = (bf16[2,2,1,32,1024]{4,3,2,1,0:T(8,128)(2,1)S(1)}, bf16[2,2,1,32,1024]{4,3,2,1,0:T(8,128)(2,1)S(1)}, u32[]{:S(2)}, u32[]{:S(2)}) collective-permute-start(bf16[2,2,1,32,1024]{4,3,2,1,0:T(8,128)(2,1)S(1)} %select_convert_fusion), channel_id=1, source_target_pairs={{0,1},{1,0},{2,3},{3,2},{4,5},{5,4},{6,7},{7,6},{8,9},{9,8},{10,11... | collective-permute-start | bytes 786440 | tf_op jit(solution)/shard_map/ppermute | solution.py:212
  182.8 13.8 %collective-permute-start.11 = (bf16[2,1,1,32,1024]{4,3,2,1,0:T(8,128)(2,1)S(1)}, bf16[2,1,1,32,1024]{4,3,2,1,0:T(8,128)(2,1)S(1)}, u32[]{:S(2)}, u32[]{:S(2)}) collective-permute-start(bf16[2,1,1,32,1024]{4,3,2,1,0:T(8,128)(2,1)S(1)} %select_convert_fusion.2), channel_id=1, source_target_pairs={{0,2},{1,3},{2,0},{3,1},{4,6},{5,7},{6,4},{7,5},{8,10},{9,11},{10,... | collective-permute-start | bytes 393224 | tf_op jit(solution)/shard_map/ppermute | solution.py:212
  196.7 32.8 %collective-permute-start.12 = (bf16[1,1,1,32,1024]{4,3,2,1,0:T(8,128)(2,1)S(1)}, bf16[1,1,1,32,1024]{4,3,2,1,0:T(8,128)(2,1)S(1)}, u32[]{:S(2)}, u32[]{:S(2)}) collective-permute-start(bf16[1,1,1,32,1024]{4,3,2,1,0:T(8,128)(2,1)S(1)} %select_convert_fusion.3), channel_id=1, source_target_pairs={{0,4},{1,5},{2,6},{3,7},{4,0},{5,1},{6,2},{7,3},{8,12},{9,13},{10,... | collective-permute-start | bytes 196616 | tf_op jit(solution)/shard_map/ppermute | solution.py:212
  219.9 16.0 %all-to-all-start.2 = ((bf16[128,16,64]{0,2,1:T(8,128)(2,1)}), bf16[128,16,64]{0,2,1:T(8,128)(2,1)S(1)}, u32[]{:S(2)}, u32[]{:S(2)}) async-start(bf16[128,16,64]{0,2,1:T(8,128)(2,1)} %bitcast.23), calls=%async_computation.2 | async-start | bytes 524288 | tf_op jit(solution)/shard_map/all_to_all | solution.py:220
Sparse Core Ops, SparseCore 0:
  42.6 139.1 all-gather.1

commit v3 on v2

--- a/solution.py
+++ b/solution.py
@@ -2,6 +2,7 @@
 import jax.numpy as jnp
 from jax import lax
 from jax.experimental import pallas as pl
+from jax.experimental.layout import Layout, with_layout_constraint
 from jax.experimental.pallas import tpu as pltpu
 from jax.sharding import PartitionSpec as P
 
@@ -12,6 +13,7 @@
 NT = (((1,), (1,)), ((), ()))
 NN = (((1,), (0,)), ((), ()))
 tile = 256
+wide = 512
 
 
 def probs_kernel(length_ref, q_ref, k_ref, out_ref, held):
@@ -59,71 +61,68 @@
     )(length, query, key_rows)
 
 
-def grads_kernel(p_ref, q_ref, g_ref, o_ref, k_ref, v_ref, kt_ref, out_ref, dk_acc, dv_acc):
+def grads_kernel(p_ref, q_ref, g_ref, o_ref, v_ref, k_ref, out_ref, dk_acc, dv_acc):
     i = pl.program_id(0)
-    keys, size = k_ref.shape
+    keys, size = v_ref.shape
     q = q_ref[...]
-    g = g_ref[...]
+    g = jnp.concatenate([g_ref[j] for j in range(g_ref.shape[0])], axis=1)
     prod = g.astype(jnp.float32) * o_ref[...].astype(jnp.float32)
-    delta = lax.dot_general(
-        jnp.ones((8, size), jnp.float32),
-        prod,
-        NT,
-        precision=lax.Precision.HIGHEST,
-        preferred_element_type=jnp.float32,
-    )[0:1, :]
+    delta = jnp.sum(prod, axis=0, keepdims=True)
 
     @pl.when(i == 0)
     def _():
         dk_acc[...] = jnp.zeros_like(dk_acc)
         dv_acc[...] = jnp.zeros_like(dv_acc)
 
-    dqt = jnp.zeros((size, tile), jnp.float32)
+    dq = jnp.zeros((size, wide), jnp.float32)
     for start in range(0, keys, tile):
         rows = pl.ds(start, tile)
         p = p_ref[rows, :]
-        dp = lax.dot_general(v_ref[rows, :], g, NT, preferred_element_type=jnp.float32)
+        dp = lax.dot_general(v_ref[rows, :], g, NN, preferred_element_type=jnp.float32)
         ds = (p.astype(jnp.float32) * (dp - delta)).astype(jnp.bfloat16)
-        dv_acc[rows, :] += lax.dot_general(p, g, NN, preferred_element_type=jnp.float32)
-        dk_acc[rows, :] += lax.dot_general(ds, q, NN, preferred_element_type=jnp.float32)
-        dqt = dqt + lax.dot_general(kt_ref[:, rows], ds, NN, preferred_element_type=jnp.float32)
-    out_ref[pl.ds(pl.multiple_of(i * tile, tile), tile), 0:size] = dqt.T.astype(out_ref.dtype)
+        dv_acc[:, rows] += lax.dot_general(g, p, NT, preferred_element_type=jnp.float32)
+        dk_acc[:, rows] += lax.dot_general(q, ds, NT, preferred_element_type=jnp.float32)
+        dq = dq + lax.dot_general(k_ref[:, rows], ds, NN, preferred_element_type=jnp.float32)
+    out_ref[0:size, pl.ds(pl.multiple_of(i * wide, wide), wide)] = dq.astype(out_ref.dtype)
 
     @pl.when(i == pl.num_programs(0) - 1)
     def _():
-        out_ref[:, size : 2 * size] = dk_acc[...].astype(out_ref.dtype)
-        out_ref[:, 2 * size :] = dv_acc[...].astype(out_ref.dtype)
-
-
-def grads_of(probs, query, upstream, saved, key_rows, value_rows, key_cols):
-    n, size = query.shape
-    part = pl.BlockSpec((tile, size), lambda i: (i, 0))
-    whole = pl.BlockSpec((n, size), lambda i: (0, 0))
+        out_ref[size : 2 * size, :] = dk_acc[...].astype(out_ref.dtype)
+        out_ref[2 * size :, :] = dv_acc[...].astype(out_ref.dtype)
+
+
+def grads_of(probs, query_cols, upstream, saved_cols, value_rows, key_cols):
+    n, size = value_rows.shape
+    each = wide // upstream.shape[2]
+    part = pl.BlockSpec((size, wide), lambda i: (0, i))
     return pl.pallas_call(
         grads_kernel,
-        grid=(n // tile,),
+        grid=(n // wide,),
         in_specs=[
-            pl.BlockSpec((n, tile), lambda i: (0, i)),
+            pl.BlockSpec((n, wide), lambda i: (0, i)),
             part,
+            pl.BlockSpec((each, size, upstream.shape[2]), lambda i: (i, 0, 0)),
             part,
-            part,
-            whole,
-            whole,
+            pl.BlockSpec((n, size), lambda i: (0, 0)),
             pl.BlockSpec((size, n), lambda i: (0, 0)),
         ],
-        out_specs=pl.BlockSpec((n, 3 * size), lambda i: (0, 0)),
-        out_shape=jax.ShapeDtypeStruct((n, 3 * size), jnp.bfloat16),
-        scratch_shapes=[pltpu.VMEM((n, size), jnp.float32), pltpu.VMEM((n, size), jnp.float32)],
+        out_specs=pl.BlockSpec((3 * size, n), lambda i: (0, 0)),
+        out_shape=jax.ShapeDtypeStruct((3 * size, n), jnp.bfloat16),
+        scratch_shapes=[pltpu.VMEM((size, n), jnp.float32), pltpu.VMEM((size, n), jnp.float32)],
         cost_estimate=pl.CostEstimate(
             flops=8 * n * n * size, bytes_accessed=2 * n * n, transcendentals=0
         ),
         name="grads",
-    )(probs, query, upstream, saved, key_rows, value_rows, key_cols)
+    )(probs, query_cols, upstream, saved_cols, value_rows, key_cols)
 
 
 def copy_for_each(shard, axis):
     copies = jnp.broadcast_to(shard, (lax.axis_size(axis), *shard.shape))
     return lax.all_to_all(copies, axis, split_axis=0, concat_axis=0, tiled=True)
+
+
+def by_rows(array):
+    return with_layout_constraint(array, Layout(major_to_minor=tuple(range(array.ndim))))
 
 
 def compute(enc_grads, hidden, final_gain, attn_out, qkv, out_weight, doc_lengths):
@@ -132,6 +131,7 @@
     task_pos = lax.axis_index("task")
     far, core = task_pos // 2, task_pos % 2
     share_cols = feature_cols // tasks
+    seq_count = lax.axis_size("seq")
     dp_count = lax.axis_size("dp")
     seq_len = qkv.shape[1]
     head_size = qkv.shape[3] // 3
@@ -151,8 +151,11 @@
     query = heads[:, :head_size]
     key_rows = heads[:, head_size : 2 * head_size]
     value_rows = heads[:, 2 * head_size :]
-    query_after, slab = lax.optimization_barrier((query, slab))
-    probs = probs_of(doc_lengths, query_after, key_rows)
+    query_cols, key_cols = heads.T[:head_size], heads.T[head_size : 2 * head_size]
+    query, key_rows, value_rows, query_cols, key_cols, slab = lax.optimization_barrier(
+        (query, key_rows, value_rows, query_cols, key_cols, slab)
+    )
+    probs = probs_of(doc_lengths, query, key_rows)
 
     terms = enc_grads[0, 0].reshape(rows, 2, 2, share_cols)
     kept = jnp.where(core == 0, terms[:, :, 0], terms[:, :, 1])
@@ -164,8 +167,8 @@
     came = lax.ppermute(theirs.astype(jnp.bfloat16), "task", far_swap)
     summed = mine + came.astype(jnp.float32)
 
-    saved_all = copy_for_each(attn_out[0], "seq")
-    saved_all = saved_all.reshape(seq_len, -1)
+    saved_all = by_rows(copy_for_each(by_rows(attn_out[0]), "seq"))
+    saved_all = by_rows(saved_all.reshape(seq_len, -1))
 
     stream = hidden[0].astype(jnp.float32)
     gain = lax.dynamic_slice_in_dim(final_gain, task_pos * share_cols, share_cols, 0)
@@ -197,7 +200,13 @@
         axis=1,
     )
 
-    resid_full, saved_all = lax.optimization_barrier((resid_full, saved_all))
+    saved_cols = lax.dynamic_slice_in_dim(
+        saved_all, lax.axis_index("seq") * head_size, head_size, 1
+    )
+    saved_cols = lax.optimization_barrier(saved_cols).T
+    resid_full, saved_all, saved_cols = lax.optimization_barrier(
+        (resid_full, saved_all, saved_cols)
+    )
     resid_cols = lax.all_to_all(resid_full, "seq", split_axis=1, concat_axis=0, tiled=True)
     grad_block = lax.dot_general(
         resid_cols, saved_all, (((0,), (0,)), ((), ())), preferred_element_type=jnp.float32
@@ -217,12 +226,10 @@
         resid_full, weight, NN, preferred_element_type=jnp.float32
     ).astype(jnp.bfloat16)
     head_grad, resid_cols = lax.optimization_barrier((head_grad, resid_cols))
-    upstream = lax.all_to_all(head_grad, "seq", split_axis=1, concat_axis=0, tiled=True)
-    saved = lax.dynamic_slice_in_dim(
-        saved_all, lax.axis_index("seq") * head_size, head_size, 1
-    )
-    qkv_grad = grads_of(probs, query, upstream, saved, key_rows, value_rows, key_rows.T)
-    return (resid[None], qkv_grad.reshape(1, seq_len, 1, 3 * head_size), weight_grad)
+    head_grad = head_grad.T.reshape(seq_count, head_size, rows)
+    upstream = lax.all_to_all(head_grad, "seq", split_axis=0, concat_axis=0, tiled=True)
+    qkv_grad = grads_of(probs, query_cols, upstream, saved_cols, value_rows, key_cols)
+    return (resid[None], qkv_grad.T.reshape(1, seq_len, 1, 3 * head_size), weight_grad)
 
 
 def solution(mesh):

time: 264 us -> 256 us (0.970)
  the two profiles are of different devices: /device:TPU:32 before, /device:TPU:2 now
where the time goes in v3:
time: 256 us; the launch traced here: 255 us
  starting transfers between devices  107 us (42%)
  waiting for transfers between devices  51.8 us (20%)
  blocking collectives  33.8 us (13%)
  Pallas kernels  23 us (9%)
  between operations  15.1 us (6%)
  local copies, waits for them, and re-layouts  12.8 us (5%)
  matrix products  8.27 us (3%)
  other arithmetic  3.63 us (1%)
    all_to_all x1, blocking collectives, compute(): lax.all_to_all(resid_full, 'seq', split_axis=1, concat_axis=0, tiled=True)  33.8 us
    ppermute x3, starting transfers between devices, compute(): came = lax.ppermute(given, 'dp', [(d, d ^ bit) for d in range(dp_count)])  31.1 us
    ppermute x3, waiting for transfers between devices, compute(): other = lax.ppermute(slab, 'dp', [(d, d ^ bit) for d in range(dp_count)])  20 us
    ppermute x1, starting transfers between devices, compute(): came = lax.ppermute(theirs.astype(jnp.bfloat16), 'task', far_swap)  16.1 us
    ppermute x3, starting transfers between devices, compute(): other = lax.ppermute(slab, 'dp', [(d, d ^ bit) for d in range(dp_count)])  13.5 us
    ppermute x1, starting transfers between devices, compute(): across = lax.ppermute(resid, 'task', far_swap)  12.2 us
    ppermute x1, starting transfers between devices, compute(): sums = (sums + lax.ppermute(sums, 'task', far_swap))[0]  12.2 us
    pallas_call x1, Pallas kernels, grads_of(): pl.pallas_call(grads_kernel, grid=(n // wide,), in_specs=[pl.BlockSpec((n...  12 us
  transfers between devices with their start and end apart: 16, of which 11 were waited for; matrix products, arithmetic and copies ran while one was open for 9% of the time, Pallas kernels for 4%

profile of v3, /device:TPU:2, one launch (start us, length us, event | category | flops | bytes accessed | tf_op | source)
XLA Modules:
  0.0 254.9 jit_solution(15706142244518191670)
XLA Ops:
  7.2 9.2 %collective-permute-start.4 = (bf16[1,1,1,32,1024]{4,3,2,1,0:T(8,128)(2,1)}, bf16[1,1,1,32,1024]{4,3,2,1,0:T(8,128)(2,1)S(1)}, u32[]{:S(2)}, u32[]{:S(2)}) collective-permute-start(bf16[1,1,1,32,1024]{4,3,2,1,0:T(8,128)(2,1)} %bitcast.100), channel_id=1, source_target_pairs={{0,4},{1,5},{2,6},{3,7},{4,0},{5,1},{6,2},{7,3},{8,12},{9,13},{10,... | collective-permute-start | bytes 196616 | tf_op jit(solution)/shard_map/ppermute | solution.py:142
  16.5 6.6 %collective-permute-done.4 = bf16[1,1,1,32,1024]{4,3,2,1,0:T(8,128)(2,1)S(1)} collective-permute-done((bf16[1,1,1,32,1024]{4,3,2,1,0:T(8,128)(2,1)}, bf16[1,1,1,32,1024]{4,3,2,1,0:T(8,128)(2,1)S(1)}, u32[]{:S(2)}, u32[]{:S(2)}) %collective-permute-start.4) | collective-permute-done | bytes 65568 | tf_op jit(solution)/shard_map/ppermute | solution.py:142
  24.0 2.4 collective-permute-start.5
  26.4 6.9 %collective-permute-done.5 = bf16[2,1,1,32,1024]{4,3,2,1,0:T(8,128)(2,1)S(1)} collective-permute-done((bf16[2,1,1,32,1024]{4,3,2,1,0:T(8,128)(2,1)S(1)}, bf16[2,1,1,32,1024]{4,3,2,1,0:T(8,128)(2,1)S(1)}, u32[]{:S(2)}, u32[]{:S(2)}) %collective-permute-start.5) | collective-permute-done | bytes 131104 | tf_op jit(solution)/shard_map/ppermute | solution.py:142
  33.4 1.9 collective-permute-start.6
  35.3 6.5 %collective-permute-done.6 = bf16[2,2,1,32,1024]{4,3,2,1,0:T(8,128)(2,1)S(1)} collective-permute-done((bf16[2,2,1,32,1024]{4,3,2,1,0:T(8,128)(2,1)S(1)}, bf16[2,2,1,32,1024]{4,3,2,1,0:T(8,128)(2,1)S(1)}, u32[]{:S(2)}, u32[]{:S(2)}) %collective-permute-start.6) | collective-permute-done | bytes 262176 | tf_op jit(solution)/shard_map/ppermute | solution.py:142
  42.7 2.5 broadcast_in_dim.22
  45.1 7.6 %all-to-all-start = ((bf16[16,128,1024]{2,1,0:T(8,128)(2,1)}), bf16[16,128,1024]{2,1,0:T(8,128)(2,1)}, u32[]{:S(2)}, u32[]{:S(2)}) async-start(bf16[16,128,1024]{2,1,0:T(8,128)(2,1)} %broadcast_in_dim.22), calls=%async_computation | async-start | bytes 8388608 | tf_op jit(solution)/shard_map/all_to_all | solution.py:121
  53.5 1.9 collective-permute-start
  55.5 1.9 collective-permute-done
  57.6 16.1 %collective-permute-start.1 = (bf16[128,1024]{0,1:T(8,128)(2,1)S(1)}, bf16[128,1024]{0,1:T(8,128)(2,1)S(1)}, u32[]{:S(2)}, u32[]{:S(2)}) collective-permute-start(bf16[128,1024]{0,1:T(8,128)(2,1)S(1)} %fusion.11), channel_id=1, source_target_pairs={{0,256},{256,0},{128,384},{384,128},{1,257},{257,1},{129,385},{385... | collective-permute-start | bytes 786440 | tf_op jit(solution)/shard_map/ppermute | solution.py:167
  74.5 11.9 %collective-permute-done.1 = bf16[128,1024]{0,1:T(8,128)(2,1)S(1)} collective-permute-done((bf16[128,1024]{0,1:T(8,128)(2,1)S(1)}, bf16[128,1024]{0,1:T(8,128)(2,1)S(1)}, u32[]{:S(2)}, u32[]{:S(2)}) %collective-permute-start.1) | collective-permute-done | bytes 262176 | tf_op jit(solution)/shard_map/ppermute | solution.py:167
  86.6 1.9 collective-permute-start.2
  89.7 12.2 %collective-permute-start.3 = (f32[1,256]{1,0:T(1,128)S(1)}, f32[1,256]{1,0:T(1,128)S(1)}, u32[]{:S(2)}, u32[]{:S(2)}) collective-permute-start(f32[1,256]{1,0:T(1,128)S(1)} %add.50), channel_id=1, source_target_pairs={{0,256},{256,0},{128,384},{384,128},{1,257},{257,1},{129,385},{385... | collective-permute-start | bytes 3080 | tf_op jit(solution)/shard_map/ppermute | solution.py:180
  101.9 1.9 collective-permute-done.3
  104.1 12.2 %collective-permute-start.8 = (bf16[128,1024]{0,1:T(8,128)(2,1)S(1)}, bf16[128,1024]{0,1:T(8,128)(2,1)S(1)}, u32[]{:S(2)}, u32[]{:S(2)}) collective-permute-start(bf16[128,1024]{0,1:T(8,128)(2,1)S(1)} %fusion.7), channel_id=1, source_target_pairs={{0,256},{256,0},{128,384},{384,128},{1,257},{257,1},{129,385},{385... | collective-permute-start | bytes 786440 | tf_op jit(solution)/shard_map/ppermute | solution.py:187
  116.4 1.9 collective-permute-start.7
  118.3 3.9 %collective-permute-done.8 = bf16[128,1024]{0,1:T(8,128)(2,1)S(1)} collective-permute-done((bf16[128,1024]{0,1:T(8,128)(2,1)S(1)}, bf16[128,1024]{0,1:T(8,128)(2,1)S(1)}, u32[]{:S(2)}, u32[]{:S(2)}) %collective-permute-start.8) | collective-permute-done | bytes 262176 | tf_op jit(solution)/shard_map/ppermute | solution.py:187
  122.2 1.9 collective-permute-start.9
  124.1 1.5 collective-permute-done.9
  125.8 1.3 constant_dynamic-slice_fusion
  127.9 33.8 %all_to_all.29 = bf16[128,16,256]{0,2,1:T(8,128)(2,1)S(1)} all-to-all(bf16[128,16,256]{0,2,1:T(8,128)(2,1)S(1)} %bitcast.88), channel_id=1, replica_groups=mesh['task'=4,'seq'=16,'dp'=8] {'seq'}, dimensions={1} | all-to-all | bytes 2097152 | tf_op jit(solution)/shard_map/all_to_all | solution.py:210
  161.9 3.6 %fusion = f32[2,2,2,32,1024]{4,3,2,1,0:T(8,128)S(1)} fusion(bf16[2,2,2,32,2048]{4,3,2,1,0:T(8,128)(2,1)S(1)} %bitcast.96, bf16[2048,1024]{1,0:T(8,128)(2,1)} %bitcast.22), kind=kOutput, calls=%fused_computation | convolution fusion | flops 1073741824 | bytes 6291456 | tf_op jit(solution)/shard_map/dot_general | solution.py:211
  165.6 14.4 %collective-permute-start.10 = (bf16[2,2,1,32,1024]{4,3,2,1,0:T(8,128)(2,1)S(1)}, bf16[2,2,1,32,1024]{4,3,2,1,0:T(8,128)(2,1)S(1)}, u32[]{:S(2)}, u32[]{:S(2)}) collective-permute-start(bf16[2,2,1,32,1024]{4,3,2,1,0:T(8,128)(2,1)S(1)} %select_convert_fusion), channel_id=1, source_target_pairs={{0,1},{1,0},{2,3},{3,2},{4,5},{5,4},{6,7},{7,6},{8,9},{9,8},{10,11... | collective-permute-start | bytes 786440 | tf_op jit(solution)/shard_map/ppermute | solution.py:221
  180.1 5.5 %collective-permute-done.10 = bf16[2,2,1,32,1024]{4,3,2,1,0:T(8,128)(2,1)S(1)} collective-permute-done((bf16[2,2,1,32,1024]{4,3,2,1,0:T(8,128)(2,1)S(1)}, bf16[2,2,1,32,1024]{4,3,2,1,0:T(8,128)(2,1)S(1)}, u32[]{:S(2)}, u32[]{:S(2)}) %collective-permute-start.10) | collective-permute-done | bytes 262176 | tf_op jit(solution)/shard_map/ppermute | solution.py:221
  185.8 1.9 collective-permute-start.11
  191.3 4.1 %collective-permute-done.11 = bf16[2,1,1,32,1024]{4,3,2,1,0:T(8,128)(2,1)S(1)} collective-permute-done((bf16[2,1,1,32,1024]{4,3,2,1,0:T(8,128)(2,1)S(1)}, bf16[2,1,1,32,1024]{4,3,2,1,0:T(8,128)(2,1)S(1)}, u32[]{:S(2)}, u32[]{:S(2)}) %collective-permute-start.11) | collective-permute-done | bytes 131104 | tf_op jit(solution)/shard_map/ppermute | solution.py:221
  195.4 14.8 %collective-permute-start.12 = (bf16[1,1,1,32,1024]{4,3,2,1,0:T(8,128)(2,1)S(1)}, bf16[1,1,1,32,1024]{4,3,2,1,0:T(8,128)(2,1)S(1)}, u32[]{:S(2)}, u32[]{:S(2)}) collective-permute-start(bf16[1,1,1,32,1024]{4,3,2,1,0:T(8,128)(2,1)S(1)} %select_convert_fusion.3), channel_id=1, source_target_pairs={{0,4},{1,5},{2,6},{3,7},{4,0},{5,1},{6,2},{7,3},{8,12},{9,13},{10,... | collective-permute-start | bytes 196616 | tf_op jit(solution)/shard_map/ppermute | solution.py:221
  210.2 4.7 %convolution_convert_fusion = bf16[128,1024]{1,0:T(8,128)(2,1)S(1)} fusion(bf16[128,4096]{0,1:T(8,128)(2,1)S(1)} %pad_maximum_fusion, bf16[4096,1024]{1,0:T(8,128)(2,1)} %all-gather.2.cloned.1.call-done), kind=kOutput, calls=%fused_computation.2 | convolution fusion | flops 1073872896 | bytes 9699328 | tf_op jit(solution)/shard_map/dot_general | solution.py:225
  215.7 6.0 %all-to-all-start.2 = ((bf16[16,64,128]{2,1,0:T(8,128)(2,1)}), bf16[16,64,128]{2,1,0:T(8,128)(2,1)S(1)}, u32[]{:S(2)}, u32[]{:S(2)}) async-start(bf16[16,64,128]{2,1,0:T(8,128)(2,1)} %bitcast.27), calls=%async_computation.2 | async-start | bytes 524288 | tf_op jit(solution)/shard_map/all_to_all | solution.py:230
  221.7 11.1 %probs.1.p_ref = bf16[2048,2048]{1,0:T(8,128)(2,1)} custom-call(s32[1]{0:T(128)S(6)} %copy.34.length_ref, bf16[2048,64]{1,0:T(8,128)(2,1)} %copy.22.q_ref, bf16[2048,64]{1,0:T(8,128)(2,1)} %copy.23.k_ref), custom_call_target="tpu_custom_call" | custom-call | flops 2147483648 | bytes 8388608 | tf_op jit(solution)/shard_map/probs/pallas_call | solution.py:46
  236.1 12.0 %grads.1 = bf16[192,2048]{1,0:T(8,128)(2,1)} custom-call(bf16[2048,2048]{1,0:T(8,128)(2,1)} %probs.1.p_ref, bf16[64,2048]{1,0:T(8,128)(2,1)} %get-tuple-element.14.q_ref, bf16[16,64,128]{2,1,0:T(8,128)(2,1)} %copy-done.2, bf16[64,2048]{1,0:T(8,128)(2,1)} %bitcast.97, bf16[2048,64]{1,0:T(8,128)(2,1)} %copy.27.v_ref, bf16[64,2048]{1,0:T(8,128)(2,1)} %get-tuple-element.19.k_ref), custom_call_target="tpu_custom_call" | custom-call | flops 2147483648 | bytes 8388608 | tf_op jit(solution)/shard_map/grads/pallas_call | solution.py:98
  (54 shorter events, 13.9 us)
Async XLA Ops:
  7.2 35.5 %copy-start.3 = (bf16[1,128,1024]{2,1,0:T(8,128)(2,1)S(1)}, bf16[1,128,1024]{2,1,0:T(8,128)(2,1)}, u32[]{:S(2)}) copy-start(bf16[1,128,1024]{2,1,0:T(8,128)(2,1)} %param.10) | copy-start | bytes 786436
  7.2 203.0 %all-gather.2.cloned.1.call-start = ((), (), s32[]{:S(2)}) async-start(), calls=%async_computation.3 | async-start | bytes 8912896 | tf_op jit(solution)/shard_map/all_gather | solution.py:148
  7.2 15.9 %collective-permute-start.4 = (bf16[1,1,1,32,1024]{4,3,2,1,0:T(8,128)(2,1)}, bf16[1,1,1,32,1024]{4,3,2,1,0:T(8,128)(2,1)S(1)}, u32[]{:S(2)}, u32[]{:S(2)}) collective-permute-start(bf16[1,1,1,32,1024]{4,3,2,1,0:T(8,128)(2,1)} %bitcast.100), channel_id=1, source_target_pairs={{0,4},{1,5},{2,6},{3,7},{4,0},{5,1},{6,2},{7,3},{8,12},{9,13},{10,... | collective-permute-start | bytes 196616 | tf_op jit(solution)/shard_map/ppermute | solution.py:142
  24.0 9.3 %collective-permute-start.5 = (bf16[2,1,1,32,1024]{4,3,2,1,0:T(8,128)(2,1)S(1)}, bf16[2,1,1,32,1024]{4,3,2,1,0:T(8,128)(2,1)S(1)}, u32[]{:S(2)}, u32[]{:S(2)}) collective-permute-start(bf16[2,1,1,32,1024]{4,3,2,1,0:T(8,128)(2,1)S(1)} %pad_maximum_fusion.3), channel_id=1, source_target_pairs={{0,2},{1,3},{2,0},{3,1},{4,6},{5,7},{6,4},{7,5},{8,10},{9,11},{10,... | collective-permute-start | bytes 393224 | tf_op jit(solution)/shard_map/ppermute | solution.py:142
  33.4 8.4 %collective-permute-start.6 = (bf16[2,2,1,32,1024]{4,3,2,1,0:T(8,128)(2,1)S(1)}, bf16[2,2,1,32,1024]{4,3,2,1,0:T(8,128)(2,1)S(1)}, u32[]{:S(2)}, u32[]{:S(2)}) collective-permute-start(bf16[2,2,1,32,1024]{4,3,2,1,0:T(8,128)(2,1)S(1)} %pad_maximum_fusion.2), channel_id=1, source_target_pairs={{0,1},{1,0},{2,3},{3,2},{4,5},{5,4},{6,7},{7,6},{8,9},{9,8},{10,11... | collective-permute-start | bytes 786440 | tf_op jit(solution)/shard_map/ppermute | solution.py:142
  45.1 7.6 %copy-start.1 = (bf16[1,1,128,4096]{3,2,1,0:T(8,128)(2,1)S(1)}, bf16[1,1,128,4096]{3,2,1,0:T(8,128)(2,1)}, u32[]{:S(2)}) copy-start(bf16[1,1,128,4096]{3,2,1,0:T(8,128)(2,1)} %param.7) | copy-start | bytes 3145732
  45.1 80.6 %all-to-all-start = ((bf16[16,128,1024]{2,1,0:T(8,128)(2,1)}), bf16[16,128,1024]{2,1,0:T(8,128)(2,1)}, u32[]{:S(2)}, u32[]{:S(2)}) async-start(bf16[16,128,1024]{2,1,0:T(8,128)(2,1)} %broadcast_in_dim.22), calls=%async_computation | async-start | bytes 8388608 | tf_op jit(solution)/shard_map/all_to_all | solution.py:121
  52.7 20.9 %copy-start.4 = (bf16[1,128,1024]{2,1,0:T(8,128)(2,1)S(1)}, bf16[1,128,1024]{2,1,0:T(8,128)(2,1)}, u32[]{:S(2)}) copy-start(bf16[1,128,1024]{2,1,0:T(8,128)(2,1)} %param.8) | copy-start | bytes 786436
  53.5 3.8 %collective-permute-start = (bf16[128,2,1024]{0,2,1:T(8,128)(2,1)S(1)}, bf16[128,2,1024]{0,2,1:T(8,128)(2,1)S(1)}, u32[]{:S(2)}, u32[]{:S(2)}) collective-permute-start(bf16[128,2,1024]{0,2,1:T(8,128)(2,1)S(1)} %fusion.8), channel_id=1, source_target_pairs={{0,128},{128,0},{256,384},{384,256},{1,129},{129,1},{257,385},{385... | collective-permute-start | bytes 1572872 | tf_op jit(solution)/shard_map/ppermute | solution.py:163
  57.6 28.9 %collective-permute-start.1 = (bf16[128,1024]{0,1:T(8,128)(2,1)S(1)}, bf16[128,1024]{0,1:T(8,128)(2,1)S(1)}, u32[]{:S(2)}, u32[]{:S(2)}) collective-permute-start(bf16[128,1024]{0,1:T(8,128)(2,1)S(1)} %fusion.11), channel_id=1, source_target_pairs={{0,256},{256,0},{128,384},{384,128},{1,257},{257,1},{129,385},{385... | collective-permute-start | bytes 786440 | tf_op jit(solution)/shard_map/ppermute | solution.py:167
  86.6 3.1 %collective-permute-start.2 = (f32[1,256]{1,0:T(1,128)S(1)}, f32[1,256]{1,0:T(1,128)S(1)}, u32[]{:S(2)}, u32[]{:S(2)}) collective-permute-start(f32[1,256]{1,0:T(1,128)S(1)} %bitcast.101), channel_id=1, source_target_pairs={{0,128},{128,0},{256,384},{384,256},{1,129},{129,1},{257,385},{385... | collective-permute-start | bytes 3080 | tf_op jit(solution)/shard_map/ppermute | solution.py:179
  89.7 14.2 %collective-permute-start.3 = (f32[1,256]{1,0:T(1,128)S(1)}, f32[1,256]{1,0:T(1,128)S(1)}, u32[]{:S(2)}, u32[]{:S(2)}) collective-permute-start(f32[1,256]{1,0:T(1,128)S(1)} %add.50), channel_id=1, source_target_pairs={{0,256},{256,0},{128,384},{384,128},{1,257},{257,1},{129,385},{385... | collective-permute-start | bytes 3080 | tf_op jit(solution)/shard_map/ppermute | solution.py:180
  104.1 18.1 %collective-permute-start.8 = (bf16[128,1024]{0,1:T(8,128)(2,1)S(1)}, bf16[128,1024]{0,1:T(8,128)(2,1)S(1)}, u32[]{:S(2)}, u32[]{:S(2)}) collective-permute-start(bf16[128,1024]{0,1:T(8,128)(2,1)S(1)} %fusion.7), channel_id=1, source_target_pairs={{0,256},{256,0},{128,384},{384,128},{1,257},{257,1},{129,385},{385... | collective-permute-start | bytes 786440 | tf_op jit(solution)/shard_map/ppermute | solution.py:187
  116.4 7.7 %collective-permute-start.7 = (bf16[128,1024]{0,1:T(8,128)(2,1)S(1)}, bf16[128,1024]{0,1:T(8,128)(2,1)S(1)}, u32[]{:S(2)}, u32[]{:S(2)}) collective-permute-start(bf16[128,1024]{0,1:T(8,128)(2,1)S(1)} %fusion.7), channel_id=1, source_target_pairs={{0,128},{128,0},{256,384},{384,256},{1,129},{129,1},{257,385},{385... | collective-permute-start | bytes 786440 | tf_op jit(solution)/shard_map/ppermute | solution.py:186
  122.2 3.4 %collective-permute-start.9 = (bf16[128,1024]{0,1:T(8,128)(2,1)S(1)}, bf16[128,1024]{0,1:T(8,128)(2,1)S(1)}, u32[]{:S(2)}, u32[]{:S(2)}) collective-permute-start(bf16[128,1024]{0,1:T(8,128)(2,1)S(1)} %collective-permute-done.8), channel_id=1, source_target_pairs={{0,128},{128,0},{256,384},{384,256},{1,129},{129,1},{257,385},{385... | collective-permute-start | bytes 786440 | tf_op jit(solution)/shard_map/ppermute | solution.py:188
  161.9 18.1 %copy-start = (bf16[1,2048,1,192]{1,3,2,0:T(8,128)(2,1)S(1)}, bf16[1,2048,1,192]{1,3,2,0:T(8,128)(2,1)}, u32[]{:S(2)}) copy-start(bf16[1,2048,1,192]{1,3,2,0:T(8,128)(2,1)} %param.11) | copy-start | bytes 2359300
  165.6 20.0 %collective-permute-start.10 = (bf16[2,2,1,32,1024]{4,3,2,1,0:T(8,128)(2,1)S(1)}, bf16[2,2,1,32,1024]{4,3,2,1,0:T(8,128)(2,1)S(1)}, u32[]{:S(2)}, u32[]{:S(2)}) collective-permute-start(bf16[2,2,1,32,1024]{4,3,2,1,0:T(8,128)(2,1)S(1)} %select_convert_fusion), channel_id=1, source_target_pairs={{0,1},{1,0},{2,3},{3,2},{4,5},{5,4},{6,7},{7,6},{8,9},{9,8},{10,11... | collective-permute-start | bytes 786440 | tf_op jit(solution)/shard_map/ppermute | solution.py:221
  185.8 9.6 %collective-permute-start.11 = (bf16[2,1,1,32,1024]{4,3,2,1,0:T(8,128)(2,1)S(1)}, bf16[2,1,1,32,1024]{4,3,2,1,0:T(8,128)(2,1)S(1)}, u32[]{:S(2)}, u32[]{:S(2)}) collective-permute-start(bf16[2,1,1,32,1024]{4,3,2,1,0:T(8,128)(2,1)S(1)} %select_convert_fusion.2), channel_id=1, source_target_pairs={{0,2},{1,3},{2,0},{3,1},{4,6},{5,7},{6,4},{7,5},{8,10},{9,11},{10,... | collective-permute-start | bytes 393224 | tf_op jit(solution)/shard_map/ppermute | solution.py:221
  195.4 39.4 %collective-permute-start.12 = (bf16[1,1,1,32,1024]{4,3,2,1,0:T(8,128)(2,1)S(1)}, bf16[1,1,1,32,1024]{4,3,2,1,0:T(8,128)(2,1)S(1)}, u32[]{:S(2)}, u32[]{:S(2)}) collective-permute-start(bf16[1,1,1,32,1024]{4,3,2,1,0:T(8,128)(2,1)S(1)} %select_convert_fusion.3), channel_id=1, source_target_pairs={{0,4},{1,5},{2,6},{3,7},{4,0},{5,1},{6,2},{7,3},{8,12},{9,13},{10,... | collective-permute-start | bytes 196616 | tf_op jit(solution)/shard_map/ppermute | solution.py:221
  215.7 19.7 %all-to-all-start.2 = ((bf16[16,64,128]{2,1,0:T(8,128)(2,1)}), bf16[16,64,128]{2,1,0:T(8,128)(2,1)S(1)}, u32[]{:S(2)}, u32[]{:S(2)}) async-start(bf16[16,64,128]{2,1,0:T(8,128)(2,1)} %bitcast.27), calls=%async_computation.2 | async-start | bytes 524288 | tf_op jit(solution)/shard_map/all_to_all | solution.py:230
  235.4 0.7 copy-start.2
Sparse Core Ops, SparseCore 0:
  42.8 139.2 all-gather.1

commit v4 on v3

--- a/solution.py
+++ b/solution.py
@@ -116,11 +116,6 @@
     )(probs, query_cols, upstream, saved_cols, value_rows, key_cols)
 
 
-def copy_for_each(shard, axis):
-    copies = jnp.broadcast_to(shard, (lax.axis_size(axis), *shard.shape))
-    return lax.all_to_all(copies, axis, split_axis=0, concat_axis=0, tiled=True)
-
-
 def by_rows(array):
     return with_layout_constraint(array, Layout(major_to_minor=tuple(range(array.ndim))))
 
@@ -152,8 +147,8 @@
     key_rows = heads[:, head_size : 2 * head_size]
     value_rows = heads[:, 2 * head_size :]
     query_cols, key_cols = heads.T[:head_size], heads.T[head_size : 2 * head_size]
-    query, key_rows, value_rows, query_cols, key_cols, slab = lax.optimization_barrier(
-        (query, key_rows, value_rows, query_cols, key_cols, slab)
+    query, key_rows, value_rows, query_cols, key_cols = lax.optimization_barrier(
+        (query, key_rows, by_rows(value_rows), query_cols, key_cols)
     )
     probs = probs_of(doc_lengths, query, key_rows)
 
@@ -167,8 +162,7 @@
     came = lax.ppermute(theirs.astype(jnp.bfloat16), "task", far_swap)
     summed = mine + came.astype(jnp.float32)
 
-    saved_all = by_rows(copy_for_each(by_rows(attn_out[0]), "seq"))
-    saved_all = by_rows(saved_all.reshape(seq_len, -1))
+    saved_all = by_rows(lax.all_gather(attn_out[0], "seq", axis=0, tiled=True))
 
     stream = hidden[0].astype(jnp.float32)
     gain = lax.dynamic_slice_in_dim(final_gain, task_pos * share_cols, share_cols, 0)

time: 256 us -> 243 us (0.949)
  blocking collectives: 33.8 us -> 27 us
  local copies, waits for them, and re-layouts: 12.8 us -> 10.2 us
    all_to_all x1 -> x0, starting transfers between devices: 7.61 us -> none  [copy_for_each(): return lax.all_to_all(copies, axis, split_axis=0, concat_axis=0, tiled=True)]
    ppermute x3, starting transfers between devices: 31.1 us -> 38.5 us  [compute(): came = lax.ppermute(given, 'dp', [(d, d ^ bit) for d in range(dp_count)])]
    all_to_all x1, blocking collectives: 33.8 us -> 27 us  [compute(): lax.all_to_all(resid_full, 'seq', split_axis=1, concat_axis=0, tiled=True)]
  transfers between devices with their start and end apart: 16 -> 16, of which waited for: 11 -> 11; matrix products, arithmetic and copies ran while one was open for 9% -> 8% of each run, Pallas kernels for 4% -> 5%
where the time goes in v4:
time: 243 us
  starting transfers between devices  106 us (44%)
  waiting for transfers between devices  51.6 us (21%)
  blocking collectives  27 us (11%)
  Pallas kernels  23 us (9%)
  between operations  15.1 us (6%)
  local copies, waits for them, and re-layouts  10.2 us (4%)
  matrix products  5.93 us (2%)
  other arithmetic  3.68 us (2%)
    ppermute x3, starting transfers between devices, compute(): came = lax.ppermute(given, 'dp', [(d, d ^ bit) for d in range(dp_count)])  38.5 us
    all_to_all x1, blocking collectives, compute(): lax.all_to_all(resid_full, 'seq', split_axis=1, concat_axis=0, tiled=True)  27 us
    ppermute x3, waiting for transfers between devices, compute(): other = lax.ppermute(slab, 'dp', [(d, d ^ bit) for d in range(dp_count)])  20 us
    ppermute x1, starting transfers between devices, compute(): came = lax.ppermute(theirs.astype(jnp.bfloat16), 'task', far_swap)  16.1 us
    ppermute x3, starting transfers between devices, compute(): other = lax.ppermute(slab, 'dp', [(d, d ^ bit) for d in range(dp_count)])  13.4 us
    ppermute x1, starting transfers between devices, compute(): across = lax.ppermute(resid, 'task', far_swap)  12.2 us
    ppermute x1, starting transfers between devices, compute(): sums = (sums + lax.ppermute(sums, 'task', far_swap))[0]  12.2 us
    pallas_call x1, Pallas kernels, grads_of(): pl.pallas_call(grads_kernel, grid=(n // wide,), in_specs=[pl.BlockSpec((n...  12 us
  transfers between devices with their start and end apart: 16, of which 11 were waited for; matrix products, arithmetic and copies ran while one was open for 8% of the time, Pallas kernels for 5%

profile of v4, /device:TPU:2, one launch (start us, length us, event | category | flops | bytes accessed | tf_op | source)
XLA Modules:
  0.0 242.7 jit_solution(7020067594735534502)
XLA Ops:
  8.0 9.1 %collective-permute-start.7 = (bf16[1,1,1,32,1024]{4,3,2,1,0:T(8,128)(2,1)}, bf16[1,1,1,32,1024]{4,3,2,1,0:T(8,128)(2,1)S(1)}, u32[]{:S(2)}, u32[]{:S(2)}) collective-permute-start(bf16[1,1,1,32,1024]{4,3,2,1,0:T(8,128)(2,1)} %bitcast.100), channel_id=1, source_target_pairs={{0,4},{1,5},{2,6},{3,7},{4,0},{5,1},{6,2},{7,3},{8,12},{9,13},{10,... | collective-permute-start | bytes 196616 | tf_op jit(solution)/shard_map/ppermute | solution.py:137
  17.1 6.6 %collective-permute-done.7 = bf16[1,1,1,32,1024]{4,3,2,1,0:T(8,128)(2,1)S(1)} collective-permute-done((bf16[1,1,1,32,1024]{4,3,2,1,0:T(8,128)(2,1)}, bf16[1,1,1,32,1024]{4,3,2,1,0:T(8,128)(2,1)S(1)}, u32[]{:S(2)}, u32[]{:S(2)}) %collective-permute-start.7) | collective-permute-done | bytes 65568 | tf_op jit(solution)/shard_map/ppermute | solution.py:137
  24.6 2.4 collective-permute-start.8
  27.0 6.9 %collective-permute-done.8 = bf16[2,1,1,32,1024]{4,3,2,1,0:T(8,128)(2,1)S(1)} collective-permute-done((bf16[2,1,1,32,1024]{4,3,2,1,0:T(8,128)(2,1)S(1)}, bf16[2,1,1,32,1024]{4,3,2,1,0:T(8,128)(2,1)S(1)}, u32[]{:S(2)}, u32[]{:S(2)}) %collective-permute-start.8) | collective-permute-done | bytes 131104 | tf_op jit(solution)/shard_map/ppermute | solution.py:137
  34.0 1.9 collective-permute-start.9
  35.9 6.5 %collective-permute-done.9 = bf16[2,2,1,32,1024]{4,3,2,1,0:T(8,128)(2,1)S(1)} collective-permute-done((bf16[2,2,1,32,1024]{4,3,2,1,0:T(8,128)(2,1)S(1)}, bf16[2,2,1,32,1024]{4,3,2,1,0:T(8,128)(2,1)S(1)}, u32[]{:S(2)}, u32[]{:S(2)}) %collective-permute-start.9) | collective-permute-done | bytes 262176 | tf_op jit(solution)/shard_map/ppermute | solution.py:137
  44.1 1.9 collective-permute-start
  46.0 1.9 collective-permute-done
  48.1 16.1 %collective-permute-start.1 = (bf16[128,1024]{0,1:T(8,128)(2,1)S(1)}, bf16[128,1024]{0,1:T(8,128)(2,1)S(1)}, u32[]{:S(2)}, u32[]{:S(2)}) collective-permute-start(bf16[128,1024]{0,1:T(8,128)(2,1)S(1)} %fusion.11), channel_id=1, source_target_pairs={{0,256},{256,0},{128,384},{384,128},{1,257},{257,1},{129,385},{385... | collective-permute-start | bytes 786440 | tf_op jit(solution)/shard_map/ppermute | solution.py:162
  65.1 11.9 %collective-permute-done.1 = bf16[128,1024]{0,1:T(8,128)(2,1)S(1)} collective-permute-done((bf16[128,1024]{0,1:T(8,128)(2,1)S(1)}, bf16[128,1024]{0,1:T(8,128)(2,1)S(1)}, u32[]{:S(2)}, u32[]{:S(2)}) %collective-permute-start.1) | collective-permute-done | bytes 262176 | tf_op jit(solution)/shard_map/ppermute | solution.py:162
  77.2 1.9 collective-permute-start.2
  79.1 1.1 collective-permute-done.2
  80.3 12.2 %collective-permute-start.3 = (f32[1,256]{1,0:T(1,128)S(1)}, f32[1,256]{1,0:T(1,128)S(1)}, u32[]{:S(2)}, u32[]{:S(2)}) collective-permute-start(f32[1,256]{1,0:T(1,128)S(1)} %add.50), channel_id=1, source_target_pairs={{0,256},{256,0},{128,384},{384,128},{1,257},{257,1},{129,385},{385... | collective-permute-start | bytes 3080 | tf_op jit(solution)/shard_map/ppermute | solution.py:174
  92.5 1.9 collective-permute-done.3
  94.7 12.2 %collective-permute-start.5 = (bf16[128,1024]{0,1:T(8,128)(2,1)S(1)}, bf16[128,1024]{0,1:T(8,128)(2,1)S(1)}, u32[]{:S(2)}, u32[]{:S(2)}) collective-permute-start(bf16[128,1024]{0,1:T(8,128)(2,1)S(1)} %fusion.7), channel_id=1, source_target_pairs={{0,256},{256,0},{128,384},{384,128},{1,257},{257,1},{129,385},{385... | collective-permute-start | bytes 786440 | tf_op jit(solution)/shard_map/ppermute | solution.py:181
  106.9 1.9 collective-permute-start.4
  108.9 3.9 %collective-permute-done.5 = bf16[128,1024]{0,1:T(8,128)(2,1)S(1)} collective-permute-done((bf16[128,1024]{0,1:T(8,128)(2,1)S(1)}, bf16[128,1024]{0,1:T(8,128)(2,1)S(1)}, u32[]{:S(2)}, u32[]{:S(2)}) %collective-permute-start.5) | collective-permute-done | bytes 262176 | tf_op jit(solution)/shard_map/ppermute | solution.py:181
  112.7 1.9 collective-permute-start.6
  114.7 1.5 collective-permute-done.6
  116.4 1.3 constant_dynamic-slice_fusion
  118.5 27.0 %all_to_all.24 = bf16[128,16,256]{0,2,1:T(8,128)(2,1)S(1)} all-to-all(bf16[128,16,256]{0,2,1:T(8,128)(2,1)S(1)} %bitcast.87), channel_id=1, replica_groups=mesh['task'=4,'seq'=16,'dp'=8] {'seq'}, dimensions={1} | all-to-all | bytes 2097152 | tf_op jit(solution)/shard_map/all_to_all | solution.py:204
  145.7 1.3 fusion
  147.0 21.8 %collective-permute-start.10 = (bf16[2,2,1,32,1024]{4,3,2,1,0:T(8,128)(2,1)S(1)}, bf16[2,2,1,32,1024]{4,3,2,1,0:T(8,128)(2,1)S(1)}, u32[]{:S(2)}, u32[]{:S(2)}) collective-permute-start(bf16[2,2,1,32,1024]{4,3,2,1,0:T(8,128)(2,1)S(1)} %select_convert_fusion), channel_id=1, source_target_pairs={{0,1},{1,0},{2,3},{3,2},{4,5},{5,4},{6,7},{7,6},{8,9},{9,8},{10,11... | collective-permute-start | bytes 786440 | tf_op jit(solution)/shard_map/ppermute | solution.py:215
  168.9 5.5 %collective-permute-done.10 = bf16[2,2,1,32,1024]{4,3,2,1,0:T(8,128)(2,1)S(1)} collective-permute-done((bf16[2,2,1,32,1024]{4,3,2,1,0:T(8,128)(2,1)S(1)}, bf16[2,2,1,32,1024]{4,3,2,1,0:T(8,128)(2,1)S(1)}, u32[]{:S(2)}, u32[]{:S(2)}) %collective-permute-start.10) | collective-permute-done | bytes 262176 | tf_op jit(solution)/shard_map/ppermute | solution.py:215
  174.6 1.9 collective-permute-start.11
  177.4 1.1 copy.22.v_ref
  181.1 3.1 %collective-permute-done.11 = bf16[2,1,1,32,1024]{4,3,2,1,0:T(8,128)(2,1)S(1)} collective-permute-done((bf16[2,1,1,32,1024]{4,3,2,1,0:T(8,128)(2,1)S(1)}, bf16[2,1,1,32,1024]{4,3,2,1,0:T(8,128)(2,1)S(1)}, u32[]{:S(2)}, u32[]{:S(2)}) %collective-permute-start.11) | collective-permute-done | bytes 131104 | tf_op jit(solution)/shard_map/ppermute | solution.py:215
  184.3 14.7 %collective-permute-start.12 = (bf16[1,1,1,32,1024]{4,3,2,1,0:T(8,128)(2,1)S(1)}, bf16[1,1,1,32,1024]{4,3,2,1,0:T(8,128)(2,1)S(1)}, u32[]{:S(2)}, u32[]{:S(2)}) collective-permute-start(bf16[1,1,1,32,1024]{4,3,2,1,0:T(8,128)(2,1)S(1)} %select_convert_fusion.3), channel_id=1, source_target_pairs={{0,4},{1,5},{2,6},{3,7},{4,0},{5,1},{6,2},{7,3},{8,12},{9,13},{10,... | collective-permute-start | bytes 196616 | tf_op jit(solution)/shard_map/ppermute | solution.py:215
  199.1 4.7 %convolution_convert_fusion = bf16[128,1024]{1,0:T(8,128)(2,1)S(1)} fusion(bf16[128,4096]{0,1:T(8,128)(2,1)S(1)} %pad_maximum_fusion, bf16[4096,1024]{1,0:T(8,128)(2,1)} %all-gather.4.cloned.1.call-done), kind=kOutput, calls=%fused_computation.2 | convolution fusion | flops 1073872896 | bytes 9699328 | tf_op jit(solution)/shard_map/dot_general | solution.py:219
  204.6 6.0 %all-to-all-start.1 = ((bf16[16,64,128]{2,1,0:T(8,128)(2,1)}), bf16[16,64,128]{2,1,0:T(8,128)(2,1)S(1)}, u32[]{:S(2)}, u32[]{:S(2)}) async-start(bf16[16,64,128]{2,1,0:T(8,128)(2,1)} %bitcast.26), calls=%async_computation.1 | async-start | bytes 524288 | tf_op jit(solution)/shard_map/all_to_all | solution.py:224
  210.6 11.1 %probs.1.p_ref = bf16[2048,2048]{1,0:T(8,128)(2,1)} custom-call(s32[1]{0:T(128)S(6)} %copy.34.length_ref, bf16[2048,64]{1,0:T(8,128)(2,1)} %copy.23.q_ref, bf16[2048,64]{1,0:T(8,128)(2,1)} %copy.24.k_ref), custom_call_target="tpu_custom_call" | custom-call | flops 2147483648 | bytes 8388608 | tf_op jit(solution)/shard_map/probs/pallas_call | solution.py:46
  223.9 12.0 %grads.1 = bf16[192,2048]{1,0:T(8,128)(2,1)} custom-call(bf16[2048,2048]{1,0:T(8,128)(2,1)} %probs.1.p_ref, bf16[64,2048]{1,0:T(8,128)(2,1)} %get-tuple-element.14.q_ref, bf16[16,64,128]{2,1,0:T(8,128)(2,1)} %copy-done.2, bf16[64,2048]{1,0:T(8,128)(2,1)} %bitcast.96, bf16[2048,64]{1,0:T(8,128)(2,1)} %copy.22.v_ref, bf16[64,2048]{1,0:T(8,128)(2,1)} %get-tuple-element.19.k_ref), custom_call_target="tpu_custom_call" | custom-call | flops 2147483648 | bytes 8388608 | tf_op jit(solution)/shard_map/grads/pallas_call | solution.py:98
  (54 shorter events, 12.4 us)
Async XLA Ops:
  7.2 36.2 %copy-start.1 = (bf16[1,1,128,4096]{3,2,1,0:T(8,128)(2,1)S(1)}, bf16[1,1,128,4096]{3,2,1,0:T(8,128)(2,1)}, u32[]{:S(2)}) copy-start(bf16[1,1,128,4096]{3,2,1,0:T(8,128)(2,1)} %param.7) | copy-start | bytes 3145732
  7.2 109.2 %all-gather.6.cloned.1.call-start = ((), (), s32[]{:S(2)}) async-start(), calls=%async_computation.3 | async-start | bytes 4456448 | tf_op jit(solution)/shard_map/all_gather | solution.py:165
  7.9 191.2 %all-gather.4.cloned.1.call-start = ((), (), s32[]{:S(2)}) async-start(), calls=%async_computation.2 | async-start | bytes 8912896 | tf_op jit(solution)/shard_map/all_gather | solution.py:143
  8.0 15.8 %collective-permute-start.7 = (bf16[1,1,1,32,1024]{4,3,2,1,0:T(8,128)(2,1)}, bf16[1,1,1,32,1024]{4,3,2,1,0:T(8,128)(2,1)S(1)}, u32[]{:S(2)}, u32[]{:S(2)}) collective-permute-start(bf16[1,1,1,32,1024]{4,3,2,1,0:T(8,128)(2,1)} %bitcast.100), channel_id=1, source_target_pairs={{0,4},{1,5},{2,6},{3,7},{4,0},{5,1},{6,2},{7,3},{8,12},{9,13},{10,... | collective-permute-start | bytes 196616 | tf_op jit(solution)/shard_map/ppermute | solution.py:137
  24.6 9.3 %collective-permute-start.8 = (bf16[2,1,1,32,1024]{4,3,2,1,0:T(8,128)(2,1)S(1)}, bf16[2,1,1,32,1024]{4,3,2,1,0:T(8,128)(2,1)S(1)}, u32[]{:S(2)}, u32[]{:S(2)}) collective-permute-start(bf16[2,1,1,32,1024]{4,3,2,1,0:T(8,128)(2,1)S(1)} %pad_maximum_fusion.3), channel_id=1, source_target_pairs={{0,2},{1,3},{2,0},{3,1},{4,6},{5,7},{6,4},{7,5},{8,10},{9,11},{10,... | collective-permute-start | bytes 393224 | tf_op jit(solution)/shard_map/ppermute | solution.py:137
  34.0 8.4 %collective-permute-start.9 = (bf16[2,2,1,32,1024]{4,3,2,1,0:T(8,128)(2,1)S(1)}, bf16[2,2,1,32,1024]{4,3,2,1,0:T(8,128)(2,1)S(1)}, u32[]{:S(2)}, u32[]{:S(2)}) collective-permute-start(bf16[2,2,1,32,1024]{4,3,2,1,0:T(8,128)(2,1)S(1)} %pad_maximum_fusion.2), channel_id=1, source_target_pairs={{0,1},{1,0},{2,3},{3,2},{4,5},{5,4},{6,7},{7,6},{8,9},{9,8},{10,11... | collective-permute-start | bytes 786440 | tf_op jit(solution)/shard_map/ppermute | solution.py:137
  42.4 21.8 %copy-start.3 = (bf16[1,128,1024]{2,1,0:T(8,128)(2,1)S(1)}, bf16[1,128,1024]{2,1,0:T(8,128)(2,1)}, u32[]{:S(2)}) copy-start(bf16[1,128,1024]{2,1,0:T(8,128)(2,1)} %param.8) | copy-start | bytes 786436
  44.1 3.8 %collective-permute-start = (bf16[128,2,1024]{0,2,1:T(8,128)(2,1)S(1)}, bf16[128,2,1024]{0,2,1:T(8,128)(2,1)S(1)}, u32[]{:S(2)}, u32[]{:S(2)}) collective-permute-start(bf16[128,2,1024]{0,2,1:T(8,128)(2,1)S(1)} %fusion.8), channel_id=1, source_target_pairs={{0,128},{128,0},{256,384},{384,256},{1,129},{129,1},{257,385},{385... | collective-permute-start | bytes 1572872 | tf_op jit(solution)/shard_map/ppermute | solution.py:158
  48.1 28.9 %collective-permute-start.1 = (bf16[128,1024]{0,1:T(8,128)(2,1)S(1)}, bf16[128,1024]{0,1:T(8,128)(2,1)S(1)}, u32[]{:S(2)}, u32[]{:S(2)}) collective-permute-start(bf16[128,1024]{0,1:T(8,128)(2,1)S(1)} %fusion.11), channel_id=1, source_target_pairs={{0,256},{256,0},{128,384},{384,128},{1,257},{257,1},{129,385},{385... | collective-permute-start | bytes 786440 | tf_op jit(solution)/shard_map/ppermute | solution.py:162
  77.2 3.1 %collective-permute-start.2 = (f32[1,256]{1,0:T(1,128)S(1)}, f32[1,256]{1,0:T(1,128)S(1)}, u32[]{:S(2)}, u32[]{:S(2)}) collective-permute-start(f32[1,256]{1,0:T(1,128)S(1)} %bitcast.101), channel_id=1, source_target_pairs={{0,128},{128,0},{256,384},{384,256},{1,129},{129,1},{257,385},{385... | collective-permute-start | bytes 3080 | tf_op jit(solution)/shard_map/ppermute | solution.py:173
  80.3 14.2 %collective-permute-start.3 = (f32[1,256]{1,0:T(1,128)S(1)}, f32[1,256]{1,0:T(1,128)S(1)}, u32[]{:S(2)}, u32[]{:S(2)}) collective-permute-start(f32[1,256]{1,0:T(1,128)S(1)} %add.50), channel_id=1, source_target_pairs={{0,256},{256,0},{128,384},{384,128},{1,257},{257,1},{129,385},{385... | collective-permute-start | bytes 3080 | tf_op jit(solution)/shard_map/ppermute | solution.py:174
  94.7 18.1 %collective-permute-start.5 = (bf16[128,1024]{0,1:T(8,128)(2,1)S(1)}, bf16[128,1024]{0,1:T(8,128)(2,1)S(1)}, u32[]{:S(2)}, u32[]{:S(2)}) collective-permute-start(bf16[128,1024]{0,1:T(8,128)(2,1)S(1)} %fusion.7), channel_id=1, source_target_pairs={{0,256},{256,0},{128,384},{384,128},{1,257},{257,1},{129,385},{385... | collective-permute-start | bytes 786440 | tf_op jit(solution)/shard_map/ppermute | solution.py:181
  106.9 7.7 %collective-permute-start.4 = (bf16[128,1024]{0,1:T(8,128)(2,1)S(1)}, bf16[128,1024]{0,1:T(8,128)(2,1)S(1)}, u32[]{:S(2)}, u32[]{:S(2)}) collective-permute-start(bf16[128,1024]{0,1:T(8,128)(2,1)S(1)} %fusion.7), channel_id=1, source_target_pairs={{0,128},{128,0},{256,384},{384,256},{1,129},{129,1},{257,385},{385... | collective-permute-start | bytes 786440 | tf_op jit(solution)/shard_map/ppermute | solution.py:180
  112.7 3.4 %collective-permute-start.6 = (bf16[128,1024]{0,1:T(8,128)(2,1)S(1)}, bf16[128,1024]{0,1:T(8,128)(2,1)S(1)}, u32[]{:S(2)}, u32[]{:S(2)}) collective-permute-start(bf16[128,1024]{0,1:T(8,128)(2,1)S(1)} %collective-permute-done.5), channel_id=1, source_target_pairs={{0,128},{128,0},{256,384},{384,256},{1,129},{129,1},{257,385},{385... | collective-permute-start | bytes 786440 | tf_op jit(solution)/shard_map/ppermute | solution.py:182
  118.5 27.2 %copy-start.4 = (bf16[1,2048,1024]{2,1,0:T(8,128)(2,1)S(1)}, bf16[1,2048,1024]{2,1,0:T(8,128)(2,1)}, u32[]{:S(2)}) copy-start(bf16[1,2048,1024]{2,1,0:T(8,128)(2,1)} %all-gather.6.cloned.1.call-done) | copy-start | bytes 12582916
  145.7 23.2 %copy-start = (bf16[1,2048,1,192]{1,3,2,0:T(8,128)(2,1)S(1)}, bf16[1,2048,1,192]{1,3,2,0:T(8,128)(2,1)}, u32[]{:S(2)}) copy-start(bf16[1,2048,1,192]{1,3,2,0:T(8,128)(2,1)} %param.11) | copy-start | bytes 2359300
  147.0 27.4 %collective-permute-start.10 = (bf16[2,2,1,32,1024]{4,3,2,1,0:T(8,128)(2,1)S(1)}, bf16[2,2,1,32,1024]{4,3,2,1,0:T(8,128)(2,1)S(1)}, u32[]{:S(2)}, u32[]{:S(2)}) collective-permute-start(bf16[2,2,1,32,1024]{4,3,2,1,0:T(8,128)(2,1)S(1)} %select_convert_fusion), channel_id=1, source_target_pairs={{0,1},{1,0},{2,3},{3,2},{4,5},{5,4},{6,7},{7,6},{8,9},{9,8},{10,11... | collective-permute-start | bytes 786440 | tf_op jit(solution)/shard_map/ppermute | solution.py:215
  174.6 9.7 %collective-permute-start.11 = (bf16[2,1,1,32,1024]{4,3,2,1,0:T(8,128)(2,1)S(1)}, bf16[2,1,1,32,1024]{4,3,2,1,0:T(8,128)(2,1)S(1)}, u32[]{:S(2)}, u32[]{:S(2)}) collective-permute-start(bf16[2,1,1,32,1024]{4,3,2,1,0:T(8,128)(2,1)S(1)} %select_convert_fusion.2), channel_id=1, source_target_pairs={{0,2},{1,3},{2,0},{3,1},{4,6},{5,7},{6,4},{7,5},{8,10},{9,11},{10,... | collective-permute-start | bytes 393224 | tf_op jit(solution)/shard_map/ppermute | solution.py:215
  184.3 38.2 %collective-permute-start.12 = (bf16[1,1,1,32,1024]{4,3,2,1,0:T(8,128)(2,1)S(1)}, bf16[1,1,1,32,1024]{4,3,2,1,0:T(8,128)(2,1)S(1)}, u32[]{:S(2)}, u32[]{:S(2)}) collective-permute-start(bf16[1,1,1,32,1024]{4,3,2,1,0:T(8,128)(2,1)S(1)} %select_convert_fusion.3), channel_id=1, source_target_pairs={{0,4},{1,5},{2,6},{3,7},{4,0},{5,1},{6,2},{7,3},{8,12},{9,13},{10,... | collective-permute-start | bytes 196616 | tf_op jit(solution)/shard_map/ppermute | solution.py:215
  204.6 18.6 %all-to-all-start.1 = ((bf16[16,64,128]{2,1,0:T(8,128)(2,1)}), bf16[16,64,128]{2,1,0:T(8,128)(2,1)S(1)}, u32[]{:S(2)}, u32[]{:S(2)}) async-start(bf16[16,64,128]{2,1,0:T(8,128)(2,1)} %bitcast.26), calls=%async_computation.1 | async-start | bytes 524288 | tf_op jit(solution)/shard_map/all_to_all | solution.py:224
  223.2 0.7 copy-start.2
Sparse Core Ops, SparseCore 0:
  11.0 71.1 all-gather.5
  85.2 89.5 all-gather.3
